TPU v7x, 32 devices: a whole 2x2x4 slice. The times are simulated.
32 devices in a mesh: dp: 2 (over x), tp: 4 (over z), cp: 4 (over y, core).
Axes of the slice: x: 2, y: 2, z: 4, core: 2. Of those that a mesh axis runs over, the one named last changes fastest.
Arguments:
- x: bfloat16 [8192, 4096], P(('dp', 'cp')), parts along dimension 0
- k_cache: bfloat16 [2048, 8, 128], P(('dp', 'cp'), 'tp'), parts along dimension 0
- v_cache: bfloat16 [2048, 8, 128], P(('dp', 'cp'), 'tp'), parts along dimension 0
- rope_table: float32 [8192, 64], P(('dp', 'cp')), parts along dimension 0
- norm_gain: bfloat16 [4096], replicated
- w_qkv: bfloat16 [4096, 14336], P(None, 'tp')
- b_qkv: bfloat16 [14336], P('tp')
- w_out: bfloat16 [12288, 4096], P('tp')
Outputs:
- output 1: bfloat16 [8192, 4096], P(('dp', 'cp')), parts along dimension 0
- output 2: bfloat16 [8192, 8, 128], P(('dp', 'cp'), 'tp'), parts along dimension 0
- output 3: bfloat16 [8192, 8, 128], P(('dp', 'cp'), 'tp'), parts along dimension 0
There are 2 independent parts. A program takes and returns all parts, laid end to end along the dimension named above; an argument that names none is the same for every part.
All inputs are finite; a program needn't handle non-finite values.
Results may differ from a plain program's by a relative error of at most 0.00443274.
Values are sent between devices in bfloat16 or wider.
A program may use at most 1 GiB of HBM per device.

v0:
```python
import jax
import jax.numpy as jnp
from jax import lax
from jax.sharding import PartitionSpec as P, NamedSharding

EPS = 1.5625e-07
MASK_VALUE = -1e30


def apply_rotary(vals, cos_t, sin_t):
    pair_count = cos_t.shape[-1]
    lead_shape = vals.shape[:-1]
    paired = vals[..., :2 * pair_count].reshape(lead_shape + (pair_count, 2))
    even_part = paired[..., 0]
    odd_part = paired[..., 1]
    turned = jnp.stack([even_part * cos_t - odd_part * sin_t, odd_part * cos_t + even_part * sin_t], axis=-1)
    return jnp.concatenate([turned.reshape(lead_shape + (2 * pair_count,)), vals[..., 2 * pair_count:]], axis=-1)


def project_new(x, rope_table, norm_gain, w_qkv, b_qkv, kv_count, head_dim):
    x_f32 = x.astype(jnp.float32)
    inv_rms = lax.rsqrt(jnp.mean(x_f32 * x_f32, axis=-1, keepdims=True) + EPS)
    hidden = (x_f32 * inv_rms * norm_gain.astype(jnp.float32)).astype(jnp.bfloat16)
    tok_rows = x.shape[0]
    group = w_qkv.shape[1] // (kv_count * head_dim) - 2
    qkv_all = jnp.dot(hidden, w_qkv, preferred_element_type=jnp.float32) + b_qkv.astype(jnp.float32)
    qkv_all = qkv_all.reshape(tok_rows, kv_count, group + 2, head_dim)
    pair_count = rope_table.shape[1] // 2
    cos_t = rope_table[:, :pair_count]
    sin_t = rope_table[:, pair_count:]
    queries = apply_rotary(qkv_all[:, :, :group], cos_t[:, None, None], sin_t[:, None, None]).astype(jnp.bfloat16)
    new_k = apply_rotary(qkv_all[:, :, group], cos_t[:, None], sin_t[:, None]).astype(jnp.bfloat16)
    new_v = qkv_all[:, :, group + 1].astype(jnp.bfloat16)
    return x_f32, queries, new_k, new_v


def local_step(x, k_cache, v_cache, rope_table, norm_gain, w_qkv, b_qkv, w_out):
    kv_local, head_dim = k_cache.shape[1], k_cache.shape[2]
    tok_rows = x.shape[0]
    x_f32, queries, new_k, new_v = project_new(x, rope_table, norm_gain, w_qkv, b_qkv, kv_local, head_dim)
    group = queries.shape[2]
    k_prefix = lax.all_gather(k_cache, 'cp')
    v_prefix = lax.all_gather(v_cache, 'cp')
    k_recent = lax.all_gather(new_k, 'cp')
    v_recent = lax.all_gather(new_v, 'cp')
    cp_size = k_prefix.shape[0]
    scale = head_dim ** -0.5
    q_pos = lax.axis_index('cp') * tok_rows + jnp.arange(tok_rows)

    def attend(carry, block):
        run_max, run_sum, weighted = carry
        kp_block, vp_block, kr_block, vr_block, source = block
        s_pref = jnp.einsum('tngd,knd->tngk', queries, kp_block, preferred_element_type=jnp.float32) * scale
        s_recent = jnp.einsum('tngd,knd->tngk', queries, kr_block, preferred_element_type=jnp.float32) * scale
        k_pos = source * tok_rows + jnp.arange(tok_rows)
        visible = (k_pos[None, :] <= q_pos[:, None])[:, None, None, :]
        s_recent = jnp.where(visible, s_recent, MASK_VALUE)
        new_max = jnp.maximum(run_max, jnp.maximum(s_pref.max(axis=-1), s_recent.max(axis=-1)))
        rescale = jnp.exp(run_max - new_max)
        p_pref = jnp.exp(s_pref - new_max[..., None])
        p_recent = jnp.exp(s_recent - new_max[..., None])
        run_sum = run_sum * rescale + p_pref.sum(axis=-1) + p_recent.sum(axis=-1)
        weighted = (weighted * rescale[..., None]
                    + jnp.einsum('tngk,knd->tngd', p_pref.astype(jnp.bfloat16), vp_block, preferred_element_type=jnp.float32)
                    + jnp.einsum('tngk,knd->tngd', p_recent.astype(jnp.bfloat16), vr_block, preferred_element_type=jnp.float32))
        return (new_max, run_sum, weighted), None

    stat_shape = (tok_rows, kv_local, group)
    start_carry = (jnp.full(stat_shape, MASK_VALUE, jnp.float32), jnp.zeros(stat_shape, jnp.float32), jnp.zeros(stat_shape + (head_dim,), jnp.float32))
    (run_max, run_sum, weighted), _ = lax.scan(attend, start_carry, (k_prefix, v_prefix, k_recent, v_recent, jnp.arange(cp_size)))
    attn = (weighted / run_sum[..., None]).astype(jnp.bfloat16).reshape(tok_rows, kv_local * group * head_dim)
    proj_part = jnp.dot(attn, w_out, preferred_element_type=jnp.float32)
    y = (x_f32 + lax.psum(proj_part, 'tp')).astype(jnp.bfloat16)
    return y, new_k, new_v


def solution(mesh):
    row_spec = P(('dp', 'cp'), None)
    cache_spec = P(('dp', 'cp'), 'tp', None)
    return jax.shard_map(local_step, mesh=mesh, in_specs=(row_spec, cache_spec, cache_spec, row_spec, P(None), P(None, 'tp'), P('tp'), P('tp', None)), out_specs=(row_spec, cache_spec, cache_spec), check_vma=False)
```

profile of v0, /device:TPU:5, one launch (start us, length us, event | category | flops | bytes accessed | tf_op | source)
XLA Modules:
  0.0 1391.8 jit_solution(1497643835093978095)
XLA Ops:
  7.2 5.1 fusion.36
  12.3 0.7 convert_element_type.50
  13.0 0.7 convert_element_type.52
  13.7 37.9 %fusion.44 = f32[1024,3584]{1,0:T(8,128)} fusion(bf16[4096,3584]{1,0:T(8,128)(2,1)} %param.15, bf16[1024,4096]{1,0:T(8,128)(2,1)} %param.10, f32[4096]{0:T(1024)S(1)} %convert_element_type.50, f32[1024]{0:T(1024)S(1)} %add_rsqrt_fusion, f32[3584]{0:T(1024)S(1)} %convert_element_type.52), kind=kOutput, calls=%fused_computation.55 | convolution fusion | flops 30085218304 | bytes 52463616 | tf_op jit(solution)/shard_map/dot_general | solution.py:26
  51.6 15.3 %copy.44 = f32[1024,3584]{0,1:T(8,128)} copy(f32[1024,3584]{1,0:T(8,128)} %fusion.44) | data formatting | bytes 29360128 | tf_op jit(solution)/shard_map/add | solution.py:26
  66.9 2.1 slice.75
  69.1 1.3 slice_bitcast_fusion
  71.6 0.7 copy-done.2
  72.4 1.0 copy.49
  73.7 4.9 slice.74
  78.6 6.6 slice.52
  85.2 0.7 copy.43
  85.9 0.7 copy.50
  86.6 7.6 copy.45
  94.2 4.6 subtract_convert_fusion
  98.9 4.0 pad_maximum_fusion.1
  102.9 1.0 copy.46
  104.0 3.8 pad_maximum_fusion
  107.7 8.7 copy.52
  116.4 7.3 all-gather.1
  123.7 7.2 all-gather
  130.9 3.3 reshape.124
  134.2 1.9 copy.54
  136.2 633.8 %while.15 = (s32[]{:T(128)}, f32[1024,2,12]{0,2,1:T(8,128)S(1)}, f32[1024,2,12]{0,2,1:T(8,128)S(1)}, f32[1024,2,12,128]{0,3,2,1:T(8,128)}, bf16[4,256,2,128]{3,1...) while((s32[]{:T(128)}, f32[1024,2,12]{0,2,1:T(8,128)S(1)}, ...), condition=%wide.region_6.7_spmd.clone, body=%wide.region_1.6_spmd.clone.sunk | while | flops 16447039488 | bytes 448151744 | solution.py:70
  136.6 0.6 dynamic_slice.52
  137.8 0.7 broadcast_compare_fusion.2
  138.5 14.6 %bitcast_reduce_fusion.2 = (f32[1024,2,12]{0,2,1:T(8,128)S(1)}, f32[2,256,1024,12]{2,1,3,0:T(8,128)}) fusion(bf16[1024,2,12,128]{3,0,2,1:T(8,128)(2,1)} %get-tuple-element.293, bf16[4,256,2,128]{3,1,0,2:T(8,128)(2,1)} %get-tuple-element.292, s32[]{:T(128)S(6)} %copy.70), kind=kOutput, calls=%fused_computation.9.clone.1 | convolution fusion | flops 1623171072 | bytes 31686660 | tf_op jit(solution)/shard_map/while/body/eval_jaxpr/tngd,knd->tngk/dot_general | solution.py:53
  153.1 37.5 %fusion.71 = (f32[1024,2,12]{0,2,1:T(8,128)S(1)}, f32[2,1024,1024,12]{2,1,3,0:T(8,128)}) fusion(pred[1024,1024]{0,1:T(8,128)(4,1)S(1)} %broadcast_compare_fusion.2, bf16[1024,2,12,128]{3,0,2,1:T(8,128)(2,1)} %get-tuple-element.293, bf16[4,1024,2,128]{3,1,2,0:T(8,128)(2,1)} %get-tuple-element.295, s32[]{:T(128)S(6)} %copy.70), kind=kOutput, calls=%fused_computation.5.clone.1 | convolution fusion | flops 6517923840 | bytes 108625920 | tf_op jit(solution)/shard_map/while/body/eval_jaxpr/tngd,knd->tngk/dot_general | solution.py:54
  190.6 10.5 fusion.73
  201.1 31.3 %fusion.72 = f32[1024,2,12]{0,2,1:T(8,128)S(1)} fusion(f32[2,1024,1024,12]{2,1,3,0:T(8,128)} %get-tuple-element.256, f32[1024,2,12]{0,2,1:T(8,128)S(1)} %maximum_maximum_fusion.2, pred[1024,1024]{0,1:T(8,128)(4,1)S(1)} %broadcast_compare_fusion.2), kind=kLoop, calls=%fused_computation.4.clone.1 | loop fusion | flops 100638720 | bytes 101908480 | tf_op jit(solution)/shard_map/while/body/eval_jaxpr/reduce_sum | solution.py:62
  232.4 40.7 %fusion.75 = f32[2,128,1024,12]{2,1,3,0:T(8,128)} fusion(f32[2,1024,1024,12]{2,1,3,0:T(8,128)} %get-tuple-element.256, f32[1024,2,12]{0,2,1:T(8,128)S(1)} %maximum_maximum_fusion.2, pred[1024,1024]{0,1:T(8,128)(4,1)S(1)} %broadcast_compare_fusion.2, bf16[4,1024,2,128]{1,3,2,0:T(8,128)(2,1)} %get-tuple-element.297, s32[]{:T(128)S(6)} %copy.70), kind=kOutput, calls=%fused_computation.6.clone.1 | convolution fusion | flops 6543114240 | bytes 114917376 | tf_op jit(solution)/shard_map/while/body/eval_jaxpr/tngk,knd->tngd/dot_general | solution.py:65
  273.1 19.0 %bitcast_add_fusion.3 = f32[1024,2,12,128]{0,3,2,1:T(8,128)} fusion(f32[2,128,1024,12]{2,1,3,0:T(8,128)} %fusion.75, f32[1024,2,12,128]{0,3,2,1:T(8,128)} %get-tuple-element.277, f32[1024,2,12]{0,2,1:T(8,128)S(1)} %get-tuple-element.259, pred[]{:T(512)S(6)} %compare.3, f32[2,256,1024,12]{2,1,3,0:T(8,128)} %get-tuple-element.257, ...), kind=kOutput, calls=%fused_computation.14.clone.1 | convolution fusion | flops 1642070016 | bytes 63307780 | tf_op jit(solution)/shard_map/while/body/eval_jaxpr/tngk,knd->tngd/dot_general | solution.py:64
  292.2 0.6 dynamic_slice.52
  293.5 0.7 broadcast_compare_fusion.2
  294.1 14.6 %bitcast_reduce_fusion.2 = (f32[1024,2,12]{0,2,1:T(8,128)S(1)}, f32[2,256,1024,12]{2,1,3,0:T(8,128)}) fusion(bf16[1024,2,12,128]{3,0,2,1:T(8,128)(2,1)} %get-tuple-element.293, bf16[4,256,2,128]{3,1,0,2:T(8,128)(2,1)} %get-tuple-element.292, s32[]{:T(128)S(6)} %copy.70), kind=kOutput, calls=%fused_computation.9.clone.1 | convolution fusion | flops 1623171072 | bytes 31686660 | tf_op jit(solution)/shard_map/while/body/eval_jaxpr/tngd,knd->tngk/dot_general | solution.py:53
  308.8 37.5 %fusion.71 = (f32[1024,2,12]{0,2,1:T(8,128)S(1)}, f32[2,1024,1024,12]{2,1,3,0:T(8,128)}) fusion(pred[1024,1024]{0,1:T(8,128)(4,1)S(1)} %broadcast_compare_fusion.2, bf16[1024,2,12,128]{3,0,2,1:T(8,128)(2,1)} %get-tuple-element.293, bf16[4,1024,2,128]{3,1,2,0:T(8,128)(2,1)} %get-tuple-element.295, s32[]{:T(128)S(6)} %copy.70), kind=kOutput, calls=%fused_computation.5.clone.1 | convolution fusion | flops 6517923840 | bytes 108625920 | tf_op jit(solution)/shard_map/while/body/eval_jaxpr/tngd,knd->tngk/dot_general | solution.py:54
  346.2 10.5 fusion.73
  356.7 31.3 %fusion.72 = f32[1024,2,12]{0,2,1:T(8,128)S(1)} fusion(f32[2,1024,1024,12]{2,1,3,0:T(8,128)} %get-tuple-element.256, f32[1024,2,12]{0,2,1:T(8,128)S(1)} %maximum_maximum_fusion.2, pred[1024,1024]{0,1:T(8,128)(4,1)S(1)} %broadcast_compare_fusion.2), kind=kLoop, calls=%fused_computation.4.clone.1 | loop fusion | flops 100638720 | bytes 101908480 | tf_op jit(solution)/shard_map/while/body/eval_jaxpr/reduce_sum | solution.py:62
  388.0 40.7 %fusion.75 = f32[2,128,1024,12]{2,1,3,0:T(8,128)} fusion(f32[2,1024,1024,12]{2,1,3,0:T(8,128)} %get-tuple-element.256, f32[1024,2,12]{0,2,1:T(8,128)S(1)} %maximum_maximum_fusion.2, pred[1024,1024]{0,1:T(8,128)(4,1)S(1)} %broadcast_compare_fusion.2, bf16[4,1024,2,128]{1,3,2,0:T(8,128)(2,1)} %get-tuple-element.297, s32[]{:T(128)S(6)} %copy.70), kind=kOutput, calls=%fused_computation.6.clone.1 | convolution fusion | flops 6543114240 | bytes 114917376 | tf_op jit(solution)/shard_map/while/body/eval_jaxpr/tngk,knd->tngd/dot_general | solution.py:65
  428.8 22.6 %bitcast_add_fusion.3 = f32[1024,2,12,128]{0,3,2,1:T(8,128)} fusion(f32[2,128,1024,12]{2,1,3,0:T(8,128)} %fusion.75, f32[1024,2,12,128]{0,3,2,1:T(8,128)} %get-tuple-element.277, f32[1024,2,12]{0,2,1:T(8,128)S(1)} %get-tuple-element.259, pred[]{:T(512)S(6)} %compare.3, f32[2,256,1024,12]{2,1,3,0:T(8,128)} %get-tuple-element.257, ...), kind=kOutput, calls=%fused_computation.14.clone.1 | convolution fusion | flops 1642070016 | bytes 63307780 | tf_op jit(solution)/shard_map/while/body/eval_jaxpr/tngk,knd->tngd/dot_general | solution.py:64
  451.4 0.6 dynamic_slice.52
  452.7 0.7 broadcast_compare_fusion.2
  453.3 14.6 %bitcast_reduce_fusion.2 = (f32[1024,2,12]{0,2,1:T(8,128)S(1)}, f32[2,256,1024,12]{2,1,3,0:T(8,128)}) fusion(bf16[1024,2,12,128]{3,0,2,1:T(8,128)(2,1)} %get-tuple-element.293, bf16[4,256,2,128]{3,1,0,2:T(8,128)(2,1)} %get-tuple-element.292, s32[]{:T(128)S(6)} %copy.70), kind=kOutput, calls=%fused_computation.9.clone.1 | convolution fusion | flops 1623171072 | bytes 31686660 | tf_op jit(solution)/shard_map/while/body/eval_jaxpr/tngd,knd->tngk/dot_general | solution.py:53
  468.0 37.5 %fusion.71 = (f32[1024,2,12]{0,2,1:T(8,128)S(1)}, f32[2,1024,1024,12]{2,1,3,0:T(8,128)}) fusion(pred[1024,1024]{0,1:T(8,128)(4,1)S(1)} %broadcast_compare_fusion.2, bf16[1024,2,12,128]{3,0,2,1:T(8,128)(2,1)} %get-tuple-element.293, bf16[4,1024,2,128]{3,1,2,0:T(8,128)(2,1)} %get-tuple-element.295, s32[]{:T(128)S(6)} %copy.70), kind=kOutput, calls=%fused_computation.5.clone.1 | convolution fusion | flops 6517923840 | bytes 108625920 | tf_op jit(solution)/shard_map/while/body/eval_jaxpr/tngd,knd->tngk/dot_general | solution.py:54
  505.5 10.5 fusion.73
  516.0 31.3 %fusion.72 = f32[1024,2,12]{0,2,1:T(8,128)S(1)} fusion(f32[2,1024,1024,12]{2,1,3,0:T(8,128)} %get-tuple-element.256, f32[1024,2,12]{0,2,1:T(8,128)S(1)} %maximum_maximum_fusion.2, pred[1024,1024]{0,1:T(8,128)(4,1)S(1)} %broadcast_compare_fusion.2), kind=kLoop, calls=%fused_computation.4.clone.1 | loop fusion | flops 100638720 | bytes 101908480 | tf_op jit(solution)/shard_map/while/body/eval_jaxpr/reduce_sum | solution.py:62
  547.3 40.7 %fusion.75 = f32[2,128,1024,12]{2,1,3,0:T(8,128)} fusion(f32[2,1024,1024,12]{2,1,3,0:T(8,128)} %get-tuple-element.256, f32[1024,2,12]{0,2,1:T(8,128)S(1)} %maximum_maximum_fusion.2, pred[1024,1024]{0,1:T(8,128)(4,1)S(1)} %broadcast_compare_fusion.2, bf16[4,1024,2,128]{1,3,2,0:T(8,128)(2,1)} %get-tuple-element.297, s32[]{:T(128)S(6)} %copy.70), kind=kOutput, calls=%fused_computation.6.clone.1 | convolution fusion | flops 6543114240 | bytes 114917376 | tf_op jit(solution)/shard_map/while/body/eval_jaxpr/tngk,knd->tngd/dot_general | solution.py:65
  588.0 22.6 %bitcast_add_fusion.3 = f32[1024,2,12,128]{0,3,2,1:T(8,128)} fusion(f32[2,128,1024,12]{2,1,3,0:T(8,128)} %fusion.75, f32[1024,2,12,128]{0,3,2,1:T(8,128)} %get-tuple-element.277, f32[1024,2,12]{0,2,1:T(8,128)S(1)} %get-tuple-element.259, pred[]{:T(512)S(6)} %compare.3, f32[2,256,1024,12]{2,1,3,0:T(8,128)} %get-tuple-element.257, ...), kind=kOutput, calls=%fused_computation.14.clone.1 | convolution fusion | flops 1642070016 | bytes 63307780 | tf_op jit(solution)/shard_map/while/body/eval_jaxpr/tngk,knd->tngd/dot_general | solution.py:64
  610.7 0.6 dynamic_slice.52
  611.9 0.7 broadcast_compare_fusion.2
  612.6 14.6 %bitcast_reduce_fusion.2 = (f32[1024,2,12]{0,2,1:T(8,128)S(1)}, f32[2,256,1024,12]{2,1,3,0:T(8,128)}) fusion(bf16[1024,2,12,128]{3,0,2,1:T(8,128)(2,1)} %get-tuple-element.293, bf16[4,256,2,128]{3,1,0,2:T(8,128)(2,1)} %get-tuple-element.292, s32[]{:T(128)S(6)} %copy.70), kind=kOutput, calls=%fused_computation.9.clone.1 | convolution fusion | flops 1623171072 | bytes 31686660 | tf_op jit(solution)/shard_map/while/body/eval_jaxpr/tngd,knd->tngk/dot_general | solution.py:53
  627.2 37.5 %fusion.71 = (f32[1024,2,12]{0,2,1:T(8,128)S(1)}, f32[2,1024,1024,12]{2,1,3,0:T(8,128)}) fusion(pred[1024,1024]{0,1:T(8,128)(4,1)S(1)} %broadcast_compare_fusion.2, bf16[1024,2,12,128]{3,0,2,1:T(8,128)(2,1)} %get-tuple-element.293, bf16[4,1024,2,128]{3,1,2,0:T(8,128)(2,1)} %get-tuple-element.295, s32[]{:T(128)S(6)} %copy.70), kind=kOutput, calls=%fused_computation.5.clone.1 | convolution fusion | flops 6517923840 | bytes 108625920 | tf_op jit(solution)/shard_map/while/body/eval_jaxpr/tngd,knd->tngk/dot_general | solution.py:54
  664.7 10.5 fusion.73
  675.2 31.3 %fusion.72 = f32[1024,2,12]{0,2,1:T(8,128)S(1)} fusion(f32[2,1024,1024,12]{2,1,3,0:T(8,128)} %get-tuple-element.256, f32[1024,2,12]{0,2,1:T(8,128)S(1)} %maximum_maximum_fusion.2, pred[1024,1024]{0,1:T(8,128)(4,1)S(1)} %broadcast_compare_fusion.2), kind=kLoop, calls=%fused_computation.4.clone.1 | loop fusion | flops 100638720 | bytes 101908480 | tf_op jit(solution)/shard_map/while/body/eval_jaxpr/reduce_sum | solution.py:62
  706.5 40.7 %fusion.75 = f32[2,128,1024,12]{2,1,3,0:T(8,128)} fusion(f32[2,1024,1024,12]{2,1,3,0:T(8,128)} %get-tuple-element.256, f32[1024,2,12]{0,2,1:T(8,128)S(1)} %maximum_maximum_fusion.2, pred[1024,1024]{0,1:T(8,128)(4,1)S(1)} %broadcast_compare_fusion.2, bf16[4,1024,2,128]{1,3,2,0:T(8,128)(2,1)} %get-tuple-element.297, s32[]{:T(128)S(6)} %copy.70), kind=kOutput, calls=%fused_computation.6.clone.1 | convolution fusion | flops 6543114240 | bytes 114917376 | tf_op jit(solution)/shard_map/while/body/eval_jaxpr/tngk,knd->tngd/dot_general | solution.py:65
  747.2 22.6 %bitcast_add_fusion.3 = f32[1024,2,12,128]{0,3,2,1:T(8,128)} fusion(f32[2,128,1024,12]{2,1,3,0:T(8,128)} %fusion.75, f32[1024,2,12,128]{0,3,2,1:T(8,128)} %get-tuple-element.277, f32[1024,2,12]{0,2,1:T(8,128)S(1)} %get-tuple-element.259, pred[]{:T(512)S(6)} %compare.3, f32[2,256,1024,12]{2,1,3,0:T(8,128)} %get-tuple-element.257, ...), kind=kOutput, calls=%fused_computation.14.clone.1 | convolution fusion | flops 1642070016 | bytes 63307780 | tf_op jit(solution)/shard_map/while/body/eval_jaxpr/tngk,knd->tngd/dot_general | solution.py:64
  770.0 9.3 divide_convert_fusion
  779.3 33.6 %fusion.48 = f32[1024,4096]{1,0:T(8,128)} fusion(bf16[1024,3072]{0,1:T(8,128)(2,1)} %bitcast.120, bf16[3072,4096]{1,0:T(8,128)(2,1)} %param.17), kind=kOutput, calls=%fused_computation.73 | convolution fusion | flops 25769803776 | bytes 48234496 | tf_op jit(solution)/shard_map/dot_general | solution.py:72
  813.0 1.1 slice.76
  814.1 1.3 slice_bitcast_fusion.2
  815.4 1.1 copy.57
  816.6 1.1 copy.56
  817.7 555.3 %all-reduce.2.cloned.1.call-done = f32[1024,4096]{1,0:T(8,128)} async-done(((f32[1024,4096]{1,0:T(8,128)}), f32[1024,4096]{1,0:T(8,128)}) %all-reduce.2.cloned.1.call-update) | async-done | bytes 16777232 | tf_op jit(solution)/shard_map/psum | solution.py:73
  1373.1 12.0 fusion.39
  (58 shorter events, 2.3 us)
Async XLA Ops:
  7.2 123.7 %all-gather.8.cloned.1.call-start = ((), (), s32[]{:S(2)}) async-start(), calls=%async_computation.2 | async-start | bytes 2621440 | tf_op jit(solution)/shard_map/all_gather | solution.py:45
  51.6 19.3 %copy-start.7 = (f32[1024,64]{0,1:T(8,128)S(1)}, f32[1024,64]{0,1:T(8,128)}, u32[]{:S(2)}) copy-start(f32[1024,64]{0,1:T(8,128)} %param.13) | copy-start | bytes 786436
  69.0 67.2 %all-gather.6.cloned.1.call-start = ((), (), s32[]{:S(2)}) async-start(), calls=%async_computation | async-start | bytes 2621440 | tf_op jit(solution)/shard_map/all_gather | solution.py:44
  70.4 1.9 copy-start.1
  70.9 14.4 %copy-start.8 = (bf16[256,2,128]{2,1,0:T(2,128)(2,1)S(1)}, bf16[256,2,128]{2,1,0:T(2,128)(2,1)}, u32[]{:S(2)}) copy-start(bf16[256,2,128]{2,1,0:T(2,128)(2,1)} %param.11) | copy-start | bytes 393220
  70.9 15.1 %copy-start.9 = (bf16[256,2,128]{2,1,0:T(2,128)(2,1)S(1)}, bf16[256,2,128]{2,1,0:T(2,128)(2,1)}, u32[]{:S(2)}) copy-start(bf16[256,2,128]{2,1,0:T(2,128)(2,1)} %param.12) | copy-start | bytes 393220
  70.9 1.5 copy-start.4
  71.6 0.7 copy-start.2
  73.4 1299.6 %all-reduce.2.cloned.1.call-start = ((), (), s32[]{:S(2)}) async-start(), calls=%async_computation.1 | async-start | bytes 33554432 | tf_op jit(solution)/shard_map/psum | solution.py:73
  94.2 9.7 copy-start
  103.9 12.5 copy-start.6
  103.9 19.7 %copy-start.5 = (bf16[256,2,128]{2,0,1:T(8,128)(2,1)S(1)}, bf16[256,2,128]{2,0,1:T(8,128)(2,1)}, u32[]{:S(2)}) copy-start(bf16[256,2,128]{2,0,1:T(8,128)(2,1)} %copy.43) | copy-start | bytes 393220
  812.9 3.6 copy-start.3
Sparse Core Ops, SparseCore 0:
  69.1 22.7 all-gather.7
  94.1 22.3 all-gather.5
  813.1 559.9 all-reduce.1
where the time goes:
time: 1400 us; the launch traced here: 1390 us
  waiting for transfers between devices  555 us (40%)
  matrix products  529 us (38%)
  other arithmetic  211 us (15%)
  local copies, waits for them, and re-layouts  63.5 us (5%)
  blocking collectives  14.5 us (1%)
  between operations  14.2 us (1%)
    psum x1, waiting for transfers between devices, local_step(): y = (x_f32 + lax.psum(proj_part, 'tp')).astype(jnp.bfloat16)  555 us
    reduce_sum x8, other arithmetic, attend(): run_sum = run_sum * rescale + p_pref.sum(axis=-1) + p_recent.sum(axis=-1)  167 us
    dot_general x4, matrix products, attend(): jnp.einsum('tngk,knd->tngd', p_recent.astype(jnp.bfloat16), vr_block, pre...  163 us
    dot_general x4, matrix products, attend(): jnp.einsum('tngd,knd->tngk', queries, kr_block, preferred_element_type=jn...  150 us
    dot_general x4, matrix products, attend(): jnp.einsum('tngk,knd->tngd', p_pref.astype(jnp.bfloat16), vp_block, prefe...  86.9 us
    dot_general x4, matrix products, attend(): jnp.einsum('tngd,knd->tngk', queries, kp_block, preferred_element_type=jn...  58.5 us
    dot_general x1, matrix products, project_new(): jnp.dot(hidden, w_qkv, preferred_element_type=jnp.float32)  37.9 us
    dot_general x1, matrix products, local_step(): proj_part = jnp.dot(attn, w_out, preferred_element_type=jnp.float32)  33.6 us
  transfers between devices with their start and end apart: 3, of which 1 were waited for; matrix products, arithmetic and copies ran while one was open for 4% of the time, Pallas kernels for 0%

commit v1 on v0

v1 whole, which is shorter than its diff:
```python
import functools
import math

import jax
import jax.numpy as jnp
from jax import lax
from jax.experimental import pallas as pl
from jax.experimental.pallas import tpu as pltpu
from jax.sharding import PartitionSpec as P

EPS = 1.5625e-07
LOW = -1e30
HEAD = 128
QUAD = 4
MESH = pl.DeviceIdType.MESH


class Plan:
    def __init__(self, tok, dim, kv, group, cache, nm, kt):
        self.tok, self.dim, self.kv, self.group, self.cache = tok, dim, kv, group, cache
        self.nm = nm
        self.mr = tok // nm
        self.kt = kt
        self.nq = kv * group // QUAD
        self.qpg = group // QUAD
        self.n = QUAD * self.mr
        self.keys = tok * 5
        self.heads = kv * group
        self.wcols = QUAD * HEAD
        self.nt = dim // self.wcols
        self.cpm = 4
        self.cc = dim // self.cpm
        self.half = self.mr // 2
        self.wt = self.nq + self.nt
        self.slots = 3
        self.owns = 2
        self.s_own = self.nq
        self.s_near = self.s_own + 1
        self.s_far = self.s_near + self.nq
        self.s_fin = self.s_far + self.nq
        self.s_out = self.s_fin + 1
        self.nseg = self.s_out + self.nt
        self.sp = self.nseg // self.cpm
        self.ob = self.s_out + self.nt // self.cpm - 1
        self.od = 9
        self.ab = self.ob + 4 * self.od
        self.ad = 9
        self.chunks = self.nm * self.cpm
        self.total = self.nseg * (self.nm - 1) + self.ab + 2 * self.ad + self.sp * (self.cpm - 1) + 1


def kernel(p, x, kc, vc, rope_in, gain, bias, wqkv, wout, y, kn, vn,
           h, ka, vt, rope, q, o_t, o, s_a, s_b, p_s, mx_a, mx_b, m_s, l_s, own, land, yst, xb, w, vb,
           x_sem, w_sem, b_sem, out_sem, cs_send, cs_recv, kv_send, kv_recv,
           rs_send, rs_recv, ag_send, ag_recv, yl_sem):
    tp = lax.axis_index('tp')
    cp = lax.axis_index('cp')
    partner = cp + 1 - 2 * lax.rem(cp, 2)
    across = lax.rem(cp + 2, 4)
    scale = HEAD ** -0.5 * math.log2(math.e)
    new0 = p.tok * (1 + cp)
    rows4 = p.tok // 4

    def wq_col(j):
        return (j // p.qpg) * (p.group + 2) * HEAD + lax.rem(j, p.qpg) * p.wcols

    def w_copy(t, kind, slot):
        j = lax.rem(t, p.wt)
        if kind == 'q':
            col = pl.multiple_of(wq_col(j), HEAD)
            return pltpu.make_async_copy(wqkv.at[:, pl.ds(col, p.wcols)], w.at[slot], w_sem.at[slot])
        col = pl.multiple_of((j - p.nq) * p.wcols, HEAD)
        return pltpu.make_async_copy(wout.at[:, pl.ds(col, p.wcols)], w.at[slot, pl.ds(0, p.heads * HEAD)], w_sem.at[slot])

    def w_start(t):
        slot = lax.rem(t, p.slots)
        j = lax.rem(t, p.wt)

        @pl.when((t < p.nm * p.wt) & (j < p.nq))
        def _():
            w_copy(t, 'q', slot).start()

        @pl.when((t < p.nm * p.wt) & (j >= p.nq))
        def _():
            w_copy(t, 'o', slot).start()

    def x_copy(r):
        rows = pl.ds(r * rows4, rows4)
        return pltpu.make_async_copy(x.at[rows], h.at[rows], x_sem.at[r])

    kv_slot = p.slots - 1

    def wkv_copy(g):
        col = g * (p.group + 2) * HEAD + p.group * HEAD
        return pltpu.make_async_copy(wqkv.at[:, pl.ds(col, 2 * HEAD)], w.at[kv_slot, :, pl.ds(g * 2 * HEAD, 2 * HEAD)], b_sem.at[g])

    x_copy(0).start()
    for g in range(p.kv):
        wkv_copy(g).start()
    rope_copy = pltpu.make_async_copy(rope_in, rope, b_sem.at[2])
    rope_copy.start()
    kc_copy = pltpu.make_async_copy(kc, ka.at[:, pl.ds(cp * p.cache, p.cache)], b_sem.at[3])
    vc_copy = pltpu.make_async_copy(vc, vt.at[:, :, pl.ds(pl.multiple_of(cp * p.cache, p.cache), p.cache)], b_sem.at[4])
    kc_copy.start()
    vc_copy.start()
    for r in range(1, 4):
        x_copy(r).start()
    w_start(0)
    w_start(1)

    barrier = pltpu.get_barrier_semaphore()
    for k in range(1, 4):
        pl.semaphore_signal(barrier, inc=1, device_id={'tp': lax.rem(tp + k, 4)}, device_id_type=MESH)
        pl.semaphore_signal(barrier, inc=1, device_id={'cp': lax.rem(cp + k, 4)}, device_id_type=MESH)
    pl.semaphore_wait(barrier, 6)

    def cache_copies(owner, peer, k):
        at = pl.multiple_of(owner * p.cache, p.cache)
        ks = ka.at[:, pl.ds(at, p.cache)]
        vs = vt.at[:, :, pl.ds(at, p.cache)]
        return (pltpu.make_async_remote_copy(ks, ks, cs_send.at[k, 0], cs_recv.at[k, 0], device_id={'cp': peer}, device_id_type=MESH),
                pltpu.make_async_remote_copy(vs, vs, cs_send.at[k, 1], cs_recv.at[k, 1], device_id={'cp': peer}, device_id_type=MESH))

    def new_copies(at, size, peer, k):
        ks = ka.at[:, pl.ds(at, size)]
        vs = vt.at[:, :, pl.ds(at, size)]
        return (pltpu.make_async_remote_copy(ks, ks, kv_send.at[k, 0], kv_recv.at[k, 0], device_id={'cp': peer}, device_id_type=MESH),
                pltpu.make_async_remote_copy(vs, vs, kv_send.at[k, 1], kv_recv.at[k, 1], device_id={'cp': peer}, device_id_type=MESH))

    kc_copy.wait()
    vc_copy.wait()
    for peer, k in ((across, 1), (partner, 0)):
        for c in cache_copies(cp, peer, k):
            c.start()

    def send_new(r):
        at = pl.multiple_of(new0 + r * rows4, rows4)

        @pl.when(cp < 2)
        def _():
            for c in new_copies(at, rows4, across, 1):
                c.start()

        @pl.when(lax.rem(cp, 2) == 0)
        def _():
            for c in new_copies(at, rows4, partner, 0):
                c.start()

    lane = lax.broadcasted_iota(jnp.int32, (1, HEAD), 1)
    even = lax.rem(lane, 2) == 0
    turned = lane < 64

    def rotate(a, rows):
        c = rope[rows, 0:HEAD]
        s = rope[rows, HEAD:2 * HEAD]
        swap = jnp.where(even, pltpu.roll(a, HEAD - 1, 1), pltpu.roll(a, 1, 1))
        return jnp.where(turned, a * c + swap * s, a)

    rope_copy.wait()
    for g in range(p.kv):
        wkv_copy(g).wait()
    nsub = max(1, rows4 // 64)
    sub = rows4 // nsub

    def kv_step(r, _):
        x_copy(r).wait()

        @pl.when(r > 0)
        def _():
            send_new(r - 1)

        def norm(b, _):
            rows = pl.ds(pl.multiple_of(r * rows4 + b * sub, sub), sub)
            v = h[rows, :].astype(jnp.float32)
            inv = lax.rsqrt(jnp.mean(v * v, axis=1, keepdims=True) + EPS)
            h[rows, :] = (v * inv * gain[...]).astype(jnp.bfloat16)
            return 0

        lax.fori_loop(0, nsub, norm, 0)
        rows = pl.ds(pl.multiple_of(r * rows4, rows4), rows4)
        at = pl.multiple_of(new0 + r * rows4, rows4)
        a = jnp.dot(h[rows, :], w[kv_slot], preferred_element_type=jnp.float32)
        for g in range(p.kv):
            col = g * (p.group + 2) * HEAD + p.group * HEAD
            key = rotate(a[:, g * 2 * HEAD:g * 2 * HEAD + HEAD] + bias[0:1, col:col + HEAD], rows)
            val = a[:, g * 2 * HEAD + HEAD:(g + 1) * 2 * HEAD] + bias[0:1, col + HEAD:col + 2 * HEAD]
            ka[g, pl.ds(at, rows4), :] = key.astype(jnp.bfloat16)
            vb[g, rows, :] = val.astype(jnp.bfloat16)
            vt[g, :, pl.ds(at, rows4)] = val.T.astype(jnp.bfloat16)
        return 0

    lax.fori_loop(0, 4, kv_step, 0)
    send_new(3)
    w_start(2)

    def out_copies():
        res = []
        for g in range(p.kv):
            cols = pl.ds(g * HEAD, HEAD)
            res.append(pltpu.make_async_copy(ka.at[g, pl.ds(new0, p.tok)], kn.at[:, cols], out_sem.at[g]))
            res.append(pltpu.make_async_copy(vb.at[g], vn.at[:, cols], out_sem.at[p.kv + g]))
        return res

    for c in out_copies():
        c.start()

    def reset(i, _):
        m_s[i] = jnp.full((8, p.n), LOW, jnp.float32)
        l_s[i] = jnp.zeros((8, p.n), jnp.float32)
        o_t[i] = jnp.zeros((HEAD, p.n), jnp.float32)
        return 0

    lax.fori_loop(0, p.nq, reset, 0)

    sb = min(256, p.kt)
    ss = min(128, p.kt)
    pk = min(256, p.kt)

    def scores(hq, off, kk, s_ref, mx, bound):
        g = hq // p.qpg
        s = lax.dot_general(ka[g, pl.ds(pl.multiple_of(off + kk, sb), sb), :], q[hq], (((1,), (1,)), ((), ())),
                            preferred_element_type=jnp.float32)
        if bound is not None:
            row = lax.rem(lax.broadcasted_iota(jnp.int32, (sb, p.n), 1), p.mr)
            key = lax.broadcasted_iota(jnp.int32, (sb, p.n), 0)
            s = jnp.where(row - key >= kk - bound, s, LOW)
        s_ref[kk:kk + sb, :] = s
        top = jnp.max(s.reshape(sb // 8, 8, p.n), axis=0)
        return top if mx is None else jnp.maximum(mx, top)

    def all_scores(hq, off, s_ref, mx_ref, bound):
        mx = None
        for kk in range(0, p.kt, sb):
            mx = scores(hq, off, kk, s_ref, mx, bound)
        mx_ref[...] = mx

    def tile(hq, off, s_ref, mx_ref, hq_n, off_n, s_next, mx_next, bound_n):
        g = hq // p.qpg
        m_old = m_s[hq, 0:1, :]
        m_new = jnp.maximum(m_old, jnp.max(mx_ref[...], axis=0, keepdims=True))
        alpha = jnp.exp2((m_old - m_new) * scale)
        m_s[hq, 0:1, :] = m_new
        mc = m_new * scale
        mx = acc = out = None
        for kk in range(0, p.kt, pk):
            for k2 in range(kk, kk + pk, sb):
                mx = scores(hq_n, off_n, k2, s_next, mx, bound_n)
            for k2 in range(kk, kk + pk, ss):
                e = jnp.exp2(s_ref[k2:k2 + ss, :] * scale - mc)
                part = jnp.sum(e.reshape(ss // 8, 8, p.n), axis=0)
                acc = part if acc is None else acc + part
                p_s[k2:k2 + ss, :] = e.astype(jnp.bfloat16)
            d = jnp.dot(vt[g, :, pl.ds(pl.multiple_of(off + kk, pk), pk)], p_s[kk:kk + pk, :], preferred_element_type=jnp.float32)
            out = d if out is None else out + d
        mx_next[...] = mx
        l_s[hq] = l_s[hq] * alpha + acc
        o_t[hq] = o_t[hq] * alpha + out

    def own_segment(m):
        pairs = p.nq // 2
        tiles = (m * p.mr + p.mr + p.kt - 1) // p.kt
        last = tiles * pairs - 1

        def bound(j):
            return m * p.mr - j * p.kt

        all_scores(0, new0, s_a, mx_a, bound(0))

        def step(u, _):
            j = u // pairs
            hq = 2 * lax.rem(u, pairs)
            un = jnp.minimum(u + 1, last)
            jn = un // pairs
            hn = 2 * lax.rem(un, pairs)
            off = new0 + j * p.kt
            tile(hq, off, s_a, mx_a, hq + 1, off, s_b, mx_b, bound(j))
            tile(hq + 1, off, s_b, mx_b, hn, new0 + jn * p.kt, s_a, mx_a, bound(jn))
            return 0

        lax.fori_loop(0, tiles * pairs, step, 0)

    def block_segment(hq, count, offset):
        @pl.when(hq == 0)
        def _():
            all_scores(hq, offset(0), s_a, mx_a, None)

        def step(b, _):
            off = offset(b)
            more = b + 1 < count
            hn = jnp.where(more, hq, jnp.minimum(hq + 1, p.nq - 1))
            on = offset(jnp.where(more, b + 1, 0))
            tile(hq, off, s_a, mx_a, hq, off + p.kt, s_b, mx_b, None)
            tile(hq, off + p.kt, s_b, mx_b, hn, on, s_a, mx_a, None)
            return 0

        lax.fori_loop(0, count, step, 0)

    near = 1 + lax.rem(cp, 2)
    far = 2 * (cp // 2)

    role_a = 3 - tp
    role_b = tp

    def chain(d, i):
        m = i // p.cpm
        j = lax.rem(i, p.cpm)
        mine = own.at[lax.rem(m, p.owns), j, pl.ds(d * p.half, p.half)]
        rows = pl.ds(pl.multiple_of(m * p.mr + d * p.half, p.half), p.half)
        cols = pl.ds(pl.multiple_of(j * p.cc, p.cc), p.cc)
        return mine, land.at[d, i], y.at[rows, cols]

    def peers(d):
        return (jnp.maximum(tp - 1, 0), jnp.minimum(tp + 1, 3)) if d == 0 else (jnp.minimum(tp + 1, 3), jnp.maximum(tp - 1, 0))

    def rs_copy(d, i):
        mine, there, _ = chain(d, i)
        return pltpu.make_async_remote_copy(mine, there, rs_send.at[d, i], rs_recv.at[d, i], device_id={'tp': peers(d)[0]}, device_id_type=MESH)

    def ag_copy(d, i, src=None):
        out = chain(d, i)[2]
        return pltpu.make_async_remote_copy(out if src is None else src, out, ag_send.at[d, i], ag_recv.at[d, i],
                                            device_id={'tp': peers(d)[1]}, device_id_type=MESH)

    def yl_copy(d, i):
        k = lax.rem(i, p.cpm)
        return pltpu.make_async_copy(yst.at[d, k], chain(d, i)[2], yl_sem.at[d, k])

    def when_due(seg, first, act):
        t = jnp.maximum(seg - first, 0)
        m = t // p.nseg
        rest = lax.rem(t, p.nseg)

        @pl.when((seg >= first) & (m < p.nm) & (lax.rem(rest, p.sp) == 0) & (rest < p.sp * p.cpm))
        def _():
            act(m * p.cpm + rest // p.sp)

    def service(seg):
        for d, role in ((0, role_a), (1, role_b)):
            def sums(i, d=d, role=role):
                mine, arrived, _ = chain(d, i)

                @pl.when(role > 0)
                def _():
                    rs_copy(d, i).wait_recv()

                @pl.when((role > 0) & (role < 3))
                def _():
                    mine[...] = mine[...] + arrived[...]

                @pl.when(role < 3)
                def _():
                    rs_copy(d, i).start()

                @pl.when(role == 3)
                def _():
                    k = lax.rem(i, p.cpm)

                    @pl.when(i >= p.cpm)
                    def _():
                        yl_copy(d, i - p.cpm).wait()
                        ag_copy(d, i - p.cpm, yst.at[d, k]).wait_send()

                    yst[d, k] = (mine[...] + arrived[...]).astype(jnp.bfloat16)
                    yl_copy(d, i).start()
                    ag_copy(d, i, yst.at[d, k]).start()

            when_due(seg, p.ob + p.od * role, sums)

        for d, role in ((0, role_a), (1, role_b)):
            def rows(i, d=d, role=role):
                @pl.when(role < 3)
                def _():
                    ag_copy(d, i).wait_recv()

                @pl.when((role < 3) & (role > 0))
                def _():
                    ag_copy(d, i).start()

            when_due(seg, p.ab + p.ad * (2 - role), rows)

    row_id = lax.broadcasted_iota(jnp.int32, (p.mr, 1), 0)
    mine_a = jnp.where(tp == 0, 1, 0)
    mine_b = jnp.where(tp == 3, 1, 0)
    take_x = jnp.where(row_id < p.half, mine_a, mine_b).astype(jnp.float32)

    def xb_copy(m):
        return pltpu.make_async_copy(x.at[pl.ds(pl.multiple_of(m * p.mr, p.mr), p.mr)], xb, b_sem.at[5])

    def segment(seg, _):
        m = seg // p.nseg
        s = lax.rem(seg, p.nseg)
        busy = m < p.nm
        rows = pl.ds(pl.multiple_of(m * p.mr, p.mr), p.mr)

        @pl.when(busy & (s < p.nq))
        def _():
            t = m * p.wt + s
            slot = lax.rem(t, p.slots)

            @pl.when(s == 0)
            def _():
                xb_copy(m).start()

            w_copy(t, 'q', slot).wait()
            a = jnp.dot(h[rows, :], w[slot], preferred_element_type=jnp.float32)
            a = a + bias[0:1, pl.ds(pl.multiple_of(wq_col(s), HEAD), p.wcols)]
            for k in range(QUAD):
                q[s, k * p.mr:(k + 1) * p.mr, :] = rotate(a[:, k * HEAD:(k + 1) * HEAD], rows).astype(jnp.bfloat16)
            w_start(t + p.slots)

        @pl.when(busy & (s == p.s_own))
        def _():
            own_segment(m)

        @pl.when(seg == p.s_near)
        def _():
            for c in cache_copies(across, partner, 1):
                c.wait_recv()
            for c in cache_copies(across, partner, 2):
                c.start()
            for k in (0, 2):
                for c in cache_copies(cp, partner, k):
                    c.wait_recv()

            @pl.when(lax.rem(cp, 2) == 1)
            def _():
                for c in new_copies(pl.multiple_of(p.tok * cp, p.tok), p.tok, partner, 0):
                    c.wait_recv()

        @pl.when(busy & (s >= p.s_near) & (s < p.s_far))
        def _():
            block_segment(s - p.s_near, near, lambda b: b * p.tok * cp)

        @pl.when((seg == p.s_far) & (cp >= 2))
        def _():
            got = pl.multiple_of(p.tok * (cp - 1), p.tok)
            for c in new_copies(got, p.tok, partner, 1):
                c.wait_recv()
            for c in new_copies(got, p.tok, partner, 2):
                c.start()
            for c in new_copies(got, p.tok, partner, 2):
                c.wait_recv()

        @pl.when(busy & (s >= p.s_far) & (s < p.s_fin) & (far > 0))
        def _():
            block_segment(s - p.s_far, far, lambda b: (1 + b) * p.tok)

        @pl.when(busy & (s == p.s_fin))
        def _():
            def finish(i, _):
                inv = 1.0 / jnp.sum(l_s[i], axis=0, keepdims=True)
                v = o_t[i] * inv
                for k in range(QUAD):
                    o[:, pl.ds(pl.multiple_of((i * QUAD + k) * HEAD, HEAD), HEAD)] = v[:, k * p.mr:(k + 1) * p.mr].T.astype(jnp.bfloat16)
                return reset(i, 0)

            lax.fori_loop(0, p.nq, finish, 0)

        @pl.when(busy & (s >= p.s_out))
        def _():
            n = s - p.s_out
            t = m * p.wt + p.nq + n
            slot = lax.rem(t, p.slots)

            @pl.when(n == 0)
            def _():
                xb_copy(m).wait()

            @pl.when((n == 0) & (m >= p.owns))
            def _():
                for d, role in ((0, role_a), (1, role_b)):
                    @pl.when(role < 3)
                    def _():
                        for j in range(p.cpm):
                            rs_copy(d, (m - p.owns) * p.cpm + j).wait_send()

            w_copy(t, 'o', slot).wait()
            a = jnp.dot(o[...], w[slot, pl.ds(0, p.heads * HEAD), :], preferred_element_type=jnp.float32)
            a = a + xb[:, pl.ds(pl.multiple_of(n * p.wcols, HEAD), p.wcols)].astype(jnp.float32) * take_x
            per = p.nt // p.cpm
            own[lax.rem(m, p.owns), n // per, :, pl.ds(pl.multiple_of(lax.rem(n, per) * p.wcols, HEAD), p.wcols)] = a
            w_start(t + p.slots)

        service(seg)
        return 0

    lax.fori_loop(0, p.total, segment, 0)

    for d, role in ((0, role_a), (1, role_b)):
        @pl.when(role < 3)
        def _():
            def last_sums(i, _):
                rs_copy(d, i).wait_send()
                return 0
            lax.fori_loop((p.nm - p.owns) * p.cpm, p.chunks, last_sums, 0)

        @pl.when((role > 0) & (role < 3))
        def _():
            def last_rows(i, _):
                ag_copy(d, i).wait_send()
                return 0
            lax.fori_loop(0, p.chunks, last_rows, 0)

        @pl.when(role == 3)
        def _():
            for k in range(p.cpm):
                i = p.chunks - p.cpm + k
                yl_copy(d, i).wait()
                ag_copy(d, i, yst.at[d, k]).wait_send()

    for c in out_copies():
        c.wait()
    for k in (0, 1):
        for c in cache_copies(cp, partner, k):
            c.wait_send()
    for c in cache_copies(across, partner, 2):
        c.wait_send()

    @pl.when(cp < 2)
    def _():
        for c in new_copies(new0, p.tok, across, 1):
            c.wait_send()

    @pl.when(lax.rem(cp, 2) == 0)
    def _():
        for c in new_copies(new0, p.tok, partner, 0):
            c.wait_send()

    @pl.when(cp >= 2)
    def _():
        for c in new_copies(pl.multiple_of(p.tok * (cp - 1), p.tok), p.tok, partner, 2):
            c.wait_send()


def build(p):
    def local_step(x, k_cache, v_cache, rope_table, norm_gain, w_qkv, b_qkv, w_out):
        pairs = rope_table.shape[1] // 2
        cos = jnp.repeat(rope_table[:, :pairs], 2, axis=1)
        sin = jnp.repeat(rope_table[:, pairs:], 2, axis=1) * jnp.tile(jnp.array([-1.0, 1.0], jnp.float32), pairs)
        fill = jnp.zeros((p.tok, HEAD - 2 * pairs), jnp.float32)
        rope = jnp.concatenate([cos, fill, sin, fill], axis=1)
        anyspace = pl.BlockSpec(memory_space=pl.ANY)
        vmem = pl.BlockSpec(memory_space=pltpu.VMEM)
        bf, f32 = jnp.bfloat16, jnp.float32
        dma = pltpu.SemaphoreType.DMA
        kvw = p.kv * HEAD
        y, kn, vn = pl.pallas_call(
            functools.partial(kernel, p),
            name='block',
            out_shape=(jax.ShapeDtypeStruct((p.tok, p.dim), bf), jax.ShapeDtypeStruct((p.tok, kvw), bf), jax.ShapeDtypeStruct((p.tok, kvw), bf)),
            in_specs=[anyspace, anyspace, anyspace, anyspace, vmem, vmem, anyspace, anyspace],
            out_specs=(anyspace, anyspace, anyspace),
            scratch_shapes=[
                pltpu.VMEM((p.tok, p.dim), bf),
                pltpu.VMEM((p.kv, p.keys, HEAD), bf),
                pltpu.VMEM((p.kv, HEAD, p.keys), bf),
                pltpu.VMEM((p.tok, 2 * HEAD), f32),
                pltpu.VMEM((p.nq, p.n, HEAD), bf),
                pltpu.VMEM((p.nq, HEAD, p.n), f32),
                pltpu.VMEM((p.mr, p.heads * HEAD), bf),
                pltpu.VMEM((p.kt, p.n), f32),
                pltpu.VMEM((p.kt, p.n), f32),
                pltpu.VMEM((p.kt, p.n), bf),
                pltpu.VMEM((8, p.n), f32),
                pltpu.VMEM((8, p.n), f32),
                pltpu.VMEM((p.nq, 8, p.n), f32),
                pltpu.VMEM((p.nq, 8, p.n), f32),
                pltpu.VMEM((p.owns, p.cpm, p.mr, p.cc), f32),
                pltpu.VMEM((2, p.chunks, p.half, p.cc), f32),
                pltpu.VMEM((2, p.cpm, p.half, p.cc), bf),
                pltpu.VMEM((p.mr, p.dim), bf),
                pltpu.VMEM((p.slots, p.dim, p.wcols), bf),
                pltpu.VMEM((p.kv, p.tok, HEAD), bf),
                dma((4,)), dma((p.slots,)), dma((6,)), dma((2 * p.kv,)),
                dma((3, 2)), dma((3, 2)), dma((3, 2)), dma((3, 2)),
                dma((2, p.chunks)), dma((2, p.chunks)), dma((2, p.chunks)), dma((2, p.chunks)), dma((2, p.cpm)),
            ],
            compiler_params=pltpu.CompilerParams(collective_id=0, has_side_effects=True, vmem_limit_bytes=66_000_000),
        )(x, k_cache.transpose(1, 0, 2), v_cache.transpose(1, 2, 0), rope, norm_gain.astype(f32).reshape(1, p.dim),
          b_qkv.astype(f32).reshape(1, -1), w_qkv, w_out)
        shape = (p.tok, p.kv, HEAD)
        return y, kn.reshape(shape), vn.reshape(shape)

    return local_step


def solution(mesh):
    row_spec = P(('dp', 'cp'), None)
    cache_spec = P(('dp', 'cp'), 'tp', None)
    p = Plan(tok=1024, dim=4096, kv=2, group=12, cache=256, nm=8, kt=512)
    return jax.shard_map(build(p), mesh=mesh, in_specs=(row_spec, cache_spec, cache_spec, row_spec, P(None), P(None, 'tp'), P('tp'), P('tp', None)),
                         out_specs=(row_spec, cache_spec, cache_spec), check_vma=False)
```

time: 1400 us -> 440 us (0.31)
  waiting for transfers between devices: 555 us -> 0 us
  matrix products: 529 us -> 0 us
  Pallas kernels: 0 us -> 417 us
  other arithmetic: 211 us -> 2.78 us
  local copies, waits for them, and re-layouts: 63.5 us -> 19.1 us
  blocking collectives: 14.5 us -> 0 us
    psum x1 -> x0, waiting for transfers between devices: 555 us -> none  [local_step(): y = (x_f32 + lax.psum(proj_part, 'tp')).astype(jnp.bfloat16)]
    dot_general x18 -> x0, matrix products: 529 us -> none  [the longest x4 163 us: attend(): jnp.einsum('tngk,knd->tngd', p_recent.astype(jnp.bfloat16), vr_block, pre...]
    pallas_call x0 -> x1, Pallas kernels: none -> 417 us  [local_step(): pl.pallas_call(functools.partial(kernel, p), name='block', out_shape=(jax...]
    reduce_sum x9 -> x0, other arithmetic: 172 us -> none  [the longest x8 167 us: attend(): run_sum = run_sum * rescale + p_pref.sum(axis=-1) + p_recent.sum(axis=-1)]
    convert_element_type x4 -> x0, other arithmetic: 22.7 us -> none  [the longest x1 12 us: local_step(): y = (x_f32 + lax.psum(proj_part, 'tp')).astype(jnp.bfloat16)]
    slice x8 -> x1, local copies, waits for them, and re-layouts: 22.9 us -> 0.99 us  [local_step(): cos = jnp.repeat(rope_table[:, :pairs], 2, axis=1)]
    add x1 -> x0, local copies, waits for them, and re-layouts: 15.3 us -> none  [project_new(): jnp.dot(hidden, w_qkv, preferred_element_type=jnp.float32)]
    all_gather x2 -> x0, blocking collectives: 14.5 us -> none  [the longest x1 7.27 us: local_step(): v_prefix = lax.all_gather(v_cache, 'cp')]
  transfers between devices with their start and end apart: 3 -> 0, of which waited for: 1 -> 0; matrix products, arithmetic and copies ran while one was open for 4% -> 0% of each run, Pallas kernels for 0% -> 0%
where the time goes in v1:
time: 440 us; the launch traced here: 439 us
  Pallas kernels  417 us (95%)
  local copies, waits for them, and re-layouts  19.1 us (4%)
    pallas_call x1, Pallas kernels, local_step(): pl.pallas_call(functools.partial(kernel, p), name='block', out_shape=(jax...  417 us
    unnamed x3, local copies, waits for them, and re-layouts  11.1 us

profile of v1, /device:TPU:5, one launch (start us, length us, event | category | flops | bytes accessed | tf_op | source)
XLA Modules:
  0.0 439.5 jit_solution(2535456495133310135)
XLA Ops:
  0.6 1.3 reshape.41.bias
  1.9 0.7 tile.2
  2.6 0.1 mul.10
  2.7 1.3 reshape.38
  4.0 1.6 copy.26
  5.6 1.7 copy.21
  7.2 1.0 fusion
  8.2 0.1 broadcast_in_dim.9
  8.3 0.2 reshape.30
  8.5 0.2 copy.24
  8.7 0.1 broadcast_in_dim.11
  8.8 0.2 reshape.31
  9.0 0.2 copy.22
  9.3 1.4 pad_maximum_fusion.rope_in
  10.8 416.9 %block.1 = (bf16[1024,4096]{1,0:T(8,128)(2,1)}, bf16[1024,256]{1,0:T(8,128)(2,1)}, bf16[1024,256]{1,0:T(8,128)(2,1)}) custom-call(bf16[1024,4096]{1,0:T(8,128)(2,1)} %x.1, bf16[2,256,128]{2,1,0:T(8,128)(2,1)} %bitcast.9, bf16[2,128,256]{2,1,0:T(8,128)(2,1)} %bitcast.10, f32[1024,256]{1,0:T(8,128)} %pad_maximum_fusion.rope_in, f32[1,4096]{1,0:T(1,128)} %bitcast.11, ...), custom_call_target="tpu_custom_call" | custom-call | tf_op jit(solution)/shard_map/block/pallas_call | solution.py:547
  427.7 2.0 reshape.36
  429.6 2.0 reshape.37
  431.6 7.9 %copy.28 = bf16[1024,4096]{1,0:T(8,128)(2,1)} copy(bf16[1024,4096]{1,0:T(8,128)(2,1)} %get-tuple-element.14) | data formatting | bytes 16777216
  (2 shorter events, 0.1 us)

commit v2 on v1

v2 whole, which is shorter than its diff:
```python
import functools
import math

import jax
import jax.numpy as jnp
from jax import lax
from jax.experimental import pallas as pl
from jax.experimental.pallas import tpu as pltpu
from jax.sharding import PartitionSpec as P

EPS = 1.5625e-07
LOW = -1e30
HEAD = 128
QUAD = 4
MESH = pl.DeviceIdType.MESH


class Plan:
    def __init__(self, tok, dim, kv, group, cache, nm, kt):
        self.tok, self.dim, self.kv, self.group, self.cache = tok, dim, kv, group, cache
        self.nm = nm
        self.mr = tok // nm
        self.np = nm // 2
        self.kt = kt
        self.nq = kv * group // QUAD
        self.qpg = group // QUAD
        self.hp = self.nq // 2
        self.n = QUAD * self.mr
        self.keys = tok * 5
        self.heads = kv * group
        self.wcols = QUAD * HEAD
        self.nt = dim // self.wcols
        self.cpm = 4
        self.per = self.nt // self.cpm
        self.cc = dim // self.cpm
        self.half = self.mr // 2
        self.owns = 2
        self.s_near = self.hp
        self.s_far = self.s_near + self.hp
        self.s_fin = self.s_far + self.hp
        self.s_out = self.s_fin + 1
        self.s_q = self.s_out + self.nt
        self.nseg = self.s_q + self.hp
        self.chunks = nm * self.cpm
        self.table([[self.s_out + self.per * (j + 1) - 1 + 3 * r for j in range(self.cpm)] for r in range(4)],
                   [[self.s_out + self.per * (j + 1) - 1 + 12 + 3 * r for j in range(self.cpm)] for r in range(3)])

    def table(self, sums, rows):
        self.sums, self.rows = sums, rows
        self.total = self.nseg * (self.nm - 1) + max(max(r) for r in sums + rows) + 1

def kernel(p, x, cache_in, rope_in, small, wqkv, wout, y, kn, vn, land,
           h, ka, vt, rope, q, o_t, o, s_a, s_b, p_s, mx_a, mx_b, m_s, l_s, own, stage, yst, xb, w, wo, vb,
           x_sem, w_sem, wo_sem, b_sem, out_sem, cs_send, cs_recv, kv_send, kv_recv,
           rs_send, rs_recv, st_sem, ag_send, ag_recv, yl_sem):
    tp = lax.axis_index('tp')
    cp = lax.axis_index('cp')
    partner = cp + 1 - 2 * lax.rem(cp, 2)
    across = lax.rem(cp + 2, 4)
    scale = HEAD ** -0.5 * math.log2(math.e)
    new0 = p.tok * (1 + cp)
    rows4 = p.tok // 4
    goff = (p.group + 2) * HEAD * p.kv

    def wq_col(j):
        return (j // p.qpg) * (p.group + 2) * HEAD + lax.rem(j, p.qpg) * p.wcols

    def wq_copy(t):
        slot = lax.rem(t, 2)
        col = pl.multiple_of(wq_col(lax.rem(t, p.nq)), HEAD)
        return pltpu.make_async_copy(wqkv.at[:, pl.ds(col, p.wcols)], w.at[slot], w_sem.at[slot])

    def wo_copy(n):
        return pltpu.make_async_copy(wout.at[:, pl.ds(pl.multiple_of(n * p.wcols, HEAD), p.wcols)], wo.at[n], wo_sem.at[n])

    def x_copy(r):
        rows = pl.ds(r * rows4, rows4)
        return pltpu.make_async_copy(x.at[rows], h.at[rows], x_sem.at[r])

    def wkv_copy(g):
        col = g * (p.group + 2) * HEAD + p.group * HEAD
        return pltpu.make_async_copy(wqkv.at[:, pl.ds(col, 2 * HEAD)], w.at[1, :, pl.ds(g * 2 * HEAD, 2 * HEAD)], b_sem.at[g])

    x_copy(0).start()
    for g in range(p.kv):
        wkv_copy(g).start()
    kc_copy = pltpu.make_async_copy(cache_in.at[0], ka.at[:, pl.ds(cp * p.cache, p.cache)], b_sem.at[3])
    vc_copy = pltpu.make_async_copy(cache_in.at[1], vb.at[:, pl.ds(0, p.cache)], b_sem.at[4])
    kc_copy.start()
    vc_copy.start()
    rope_copy = pltpu.make_async_copy(rope_in, rope, b_sem.at[2])
    rope_copy.start()
    for r in range(1, 4):
        x_copy(r).start()
    wq_copy(0).start()

    barrier = pltpu.get_barrier_semaphore()
    for k in range(1, 4):
        pl.semaphore_signal(barrier, inc=1, device_id={'tp': lax.rem(tp + k, 4)}, device_id_type=MESH)
        pl.semaphore_signal(barrier, inc=1, device_id={'cp': lax.rem(cp + k, 4)}, device_id_type=MESH)

    def cache_copies(owner, peer, k):
        at = pl.multiple_of(owner * p.cache, p.cache)
        ks = ka.at[:, pl.ds(at, p.cache)]
        vs = vt.at[:, :, pl.ds(at, p.cache)]
        return (pltpu.make_async_remote_copy(ks, ks, cs_send.at[k, 0], cs_recv.at[k, 0], device_id={'cp': peer}, device_id_type=MESH),
                pltpu.make_async_remote_copy(vs, vs, cs_send.at[k, 1], cs_recv.at[k, 1], device_id={'cp': peer}, device_id_type=MESH))

    def new_copies(at, size, peer, k):
        ks = ka.at[:, pl.ds(at, size)]
        vs = vt.at[:, :, pl.ds(at, size)]
        return (pltpu.make_async_remote_copy(ks, ks, kv_send.at[k, 0], kv_recv.at[k, 0], device_id={'cp': peer}, device_id_type=MESH),
                pltpu.make_async_remote_copy(vs, vs, kv_send.at[k, 1], kv_recv.at[k, 1], device_id={'cp': peer}, device_id_type=MESH))

    vc_copy.wait()
    for g in range(p.kv):
        vt[g, :, pl.ds(pl.multiple_of(cp * p.cache, p.cache), p.cache)] = vb[g, 0:p.cache, :].astype(jnp.float32).T.astype(jnp.bfloat16)
    kc_copy.wait()
    pl.semaphore_wait(barrier, 6)
    for peer, k in ((across, 1), (partner, 0)):
        for c in cache_copies(cp, peer, k):
            c.start()

    def send_new(r):
        at = pl.multiple_of(new0 + r * rows4, rows4)

        @pl.when(cp < 2)
        def _():
            for c in new_copies(at, rows4, across, 1):
                c.start()

        @pl.when(lax.rem(cp, 2) == 0)
        def _():
            for c in new_copies(at, rows4, partner, 0):
                c.start()

    lane = lax.broadcasted_iota(jnp.int32, (1, HEAD), 1)
    even = lax.rem(lane, 2) == 0
    turned = lane < 64

    def angles(rows, count):
        r = rope[rows, :]
        both = jnp.concatenate([r, r], axis=1)
        at = lax.broadcasted_iota(jnp.int32, (count, HEAD), 1)
        pair = lax.rem(at, 64) // 2
        c = jnp.take_along_axis(both, pair, axis=1)
        s = jnp.take_along_axis(both, pair + 32, axis=1)
        return c, jnp.where(even, -s, s)

    def rotate(a, c, s):
        swap = jnp.where(even, pltpu.roll(a, HEAD - 1, 1), pltpu.roll(a, 1, 1))
        return jnp.where(turned, a * c + swap * s, a)

    rope_copy.wait()
    for g in range(p.kv):
        wkv_copy(g).wait()
    nsub = max(1, rows4 // 64)
    sub = rows4 // nsub

    def kv_step(r, _):
        x_copy(r).wait()

        @pl.when(r > 0)
        def _():
            send_new(r - 1)

        def norm(b, _):
            rows = pl.ds(pl.multiple_of(r * rows4 + b * sub, sub), sub)
            v = h[rows, :].astype(jnp.float32)
            inv = lax.rsqrt(jnp.mean(v * v, axis=1, keepdims=True) + EPS)
            h[rows, :] = (v * inv * small[0:1, goff:goff + p.dim]).astype(jnp.bfloat16)
            return 0

        lax.fori_loop(0, nsub, norm, 0)
        rows = pl.ds(pl.multiple_of(r * rows4, rows4), rows4)
        at = pl.multiple_of(new0 + r * rows4, rows4)
        a = jnp.dot(h[rows, :], w[1], preferred_element_type=jnp.float32)
        c, s = angles(rows, rows4)
        for g in range(p.kv):
            col = g * (p.group + 2) * HEAD + p.group * HEAD
            key = rotate(a[:, g * 2 * HEAD:g * 2 * HEAD + HEAD] + small[0:1, col:col + HEAD], c, s)
            val = a[:, g * 2 * HEAD + HEAD:(g + 1) * 2 * HEAD] + small[0:1, col + HEAD:col + 2 * HEAD]
            ka[g, pl.ds(at, rows4), :] = key.astype(jnp.bfloat16)
            vb[g, rows, :] = val.astype(jnp.bfloat16)
            vt[g, :, pl.ds(at, rows4)] = val.T.astype(jnp.bfloat16)
        return 0

    lax.fori_loop(0, 4, kv_step, 0)
    send_new(3)
    wq_copy(1).start()

    def out_copies():
        res = []
        for g in range(p.kv):
            cols = pl.ds(g * HEAD, HEAD)
            res.append(pltpu.make_async_copy(ka.at[g, pl.ds(new0, p.tok)], kn.at[:, cols], out_sem.at[g]))
            res.append(pltpu.make_async_copy(vb.at[g], vn.at[:, cols], out_sem.at[p.kv + g]))
        return res

    for c in out_copies():
        c.start()

    def reset(i, _):
        m_s[i] = jnp.full((8, p.n), LOW, jnp.float32)
        l_s[i] = jnp.zeros((8, p.n), jnp.float32)
        o_t[i] = jnp.zeros((HEAD, p.n), jnp.float32)
        return 0

    lax.fori_loop(0, p.nq, reset, 0)

    def q_tile(t):
        pair = t // p.nq
        j = lax.rem(t, p.nq)
        rows = pl.ds(pl.multiple_of(pair * 2 * p.mr, 2 * p.mr), 2 * p.mr)
        wq_copy(t).wait()
        a = jnp.dot(h[rows, :], w[lax.rem(t, 2)], preferred_element_type=jnp.float32)
        a = a + small[0:1, pl.ds(pl.multiple_of(wq_col(j), HEAD), p.wcols)]
        c, s = angles(rows, 2 * p.mr)
        for k in range(QUAD):
            b = rotate(a[:, k * HEAD:(k + 1) * HEAD], c, s).astype(jnp.bfloat16)
            for u in range(2):
                q[2 * lax.rem(pair, 2) + u, j, k * p.mr:(k + 1) * p.mr, :] = b[u * p.mr:(u + 1) * p.mr, :]

        @pl.when(t + 2 < p.np * p.nq)
        def _():
            wq_copy(t + 2).start()

    sb = min(256, p.kt)
    ss = min(128, p.kt)
    pk = min(256, p.kt)

    def scores(qs, hq, off, kk, s_ref, mx, bound):
        g = hq // p.qpg
        s = lax.dot_general(ka[g, pl.ds(pl.multiple_of(off + kk, sb), sb), :], q[qs, hq], (((1,), (1,)), ((), ())),
                            preferred_element_type=jnp.float32) * scale
        if bound is not None:
            row = lax.rem(lax.broadcasted_iota(jnp.int32, (sb, p.n), 1), p.mr)
            key = lax.broadcasted_iota(jnp.int32, (sb, p.n), 0)
            s = jnp.where(row - key >= kk - bound, s, LOW)
        s_ref[kk:kk + sb, :] = s
        top = jnp.max(s.reshape(sb // 8, 8, p.n), axis=0)
        return top if mx is None else jnp.maximum(mx, top)

    def all_scores(qs, hq, off, s_ref, mx_ref, bound):
        mx = None
        for kk in range(0, p.kt, sb):
            mx = scores(qs, hq, off, kk, s_ref, mx, bound)
        mx_ref[...] = mx

    def tile(qs, hq, off, s_ref, mx_ref, hq_n, off_n, s_next, mx_next, bound_n):
        g = hq // p.qpg
        m_old = m_s[hq, 0:1, :]
        m_new = jnp.maximum(m_old, jnp.max(mx_ref[...], axis=0, keepdims=True))
        alpha = jnp.exp2(m_old - m_new)
        m_s[hq, 0:1, :] = m_new
        mx = acc = out = None
        for kk in range(0, p.kt, pk):
            for k2 in range(kk, kk + pk, sb):
                mx = scores(qs, hq_n, off_n, k2, s_next, mx, bound_n)
            for k2 in range(kk, kk + pk, ss):
                e = jnp.exp2(s_ref[k2:k2 + ss, :] - m_new)
                part = jnp.sum(e.reshape(ss // 8, 8, p.n), axis=0)
                acc = part if acc is None else acc + part
                p_s[k2:k2 + ss, :] = e.astype(jnp.bfloat16)
            d = jnp.dot(vt[g, :, pl.ds(pl.multiple_of(off + kk, pk), pk)], p_s[kk:kk + pk, :], preferred_element_type=jnp.float32)
            out = d if out is None else out + d
        mx_next[...] = mx
        l_s[hq] = l_s[hq] * alpha + acc
        o_t[hq] = o_t[hq] * alpha + out

    def own_segment(u, i):
        qs = lax.rem(u, 4)
        tiles = (u * p.mr + p.mr + p.kt - 1) // p.kt
        h0 = 2 * i

        def bound(j):
            return u * p.mr - j * p.kt

        @pl.when(i == 0)
        def _():
            all_scores(qs, 0, new0, s_a, mx_a, bound(0))

        def step(j, _):
            more = j + 1 < tiles
            hn = jnp.where(more, h0, jnp.minimum(h0 + 2, p.nq - 2))
            jn = jnp.where(more, j + 1, 0)
            off = new0 + j * p.kt
            tile(qs, h0, off, s_a, mx_a, h0 + 1, off, s_b, mx_b, bound(j))
            tile(qs, h0 + 1, off, s_b, mx_b, hn, new0 + jn * p.kt, s_a, mx_a, bound(jn))
            return 0

        lax.fori_loop(0, tiles, step, 0)

    def block_segment(u, i, count, offset):
        qs = lax.rem(u, 4)
        h0 = 2 * i

        @pl.when(i == 0)
        def _():
            all_scores(qs, 0, offset(0), s_a, mx_a, None)

        def step(b, _):
            off = offset(b)
            more = b + 1 < count
            hn = jnp.where(more, h0, jnp.minimum(h0 + 2, p.nq - 2))
            on = offset(jnp.where(more, b + 1, 0))
            tile(qs, h0, off, s_a, mx_a, h0, off + p.kt, s_b, mx_b, None)
            tile(qs, h0, off + p.kt, s_b, mx_b, h0 + 1, off, s_a, mx_a, None)
            tile(qs, h0 + 1, off, s_a, mx_a, h0 + 1, off + p.kt, s_b, mx_b, None)
            tile(qs, h0 + 1, off + p.kt, s_b, mx_b, hn, on, s_a, mx_a, None)
            return 0

        lax.fori_loop(0, count, step, 0)

    near = 1 + lax.rem(cp, 2)
    far = 2 * (cp // 2)

    role_a = 3 - tp
    role_b = tp

    def chain(d, i):
        m = i // p.cpm
        j = lax.rem(i, p.cpm)
        mine = own.at[lax.rem(m, p.owns), j, pl.ds(d * p.half, p.half)]
        rows = pl.ds(pl.multiple_of(m * p.mr + d * p.half, p.half), p.half)
        cols = pl.ds(pl.multiple_of(j * p.cc, p.cc), p.cc)
        return mine, land.at[d, i], y.at[rows, cols]

    def peers(d):
        return (jnp.maximum(tp - 1, 0), jnp.minimum(tp + 1, 3)) if d == 0 else (jnp.minimum(tp + 1, 3), jnp.maximum(tp - 1, 0))

    def rs_copy(d, i):
        mine, there, _ = chain(d, i)
        return pltpu.make_async_remote_copy(mine, there, rs_send.at[d, i], rs_recv.at[d, i], device_id={'tp': peers(d)[0]}, device_id_type=MESH)

    def st_copy(d, i):
        k = lax.rem(i, 2)
        return pltpu.make_async_copy(land.at[d, i], stage.at[d, k], st_sem.at[d, k])

    def ag_copy(d, i, src=None):
        out = chain(d, i)[2]
        return pltpu.make_async_remote_copy(out if src is None else src, out, ag_send.at[d, i], ag_recv.at[d, i],
                                            device_id={'tp': peers(d)[1]}, device_id_type=MESH)

    def yl_copy(d, i):
        k = lax.rem(i, p.cpm)
        return pltpu.make_async_copy(yst.at[d, k], chain(d, i)[2], yl_sem.at[d, k])

    def pick(role, table, j):
        v = table[0][j]
        for r in range(1, len(table)):
            v = jnp.where(role == r, table[r][j], v)
        return v

    def when_due(seg, role, table, ahead, act):
        hit = seg < 0
        i = 0
        for j in range(p.cpm):
            t = seg + ahead - pick(role, table, j)
            m = jnp.maximum(t, 0) // p.nseg
            due = (t >= 0) & (m < p.nm) & (lax.rem(jnp.maximum(t, 0), p.nseg) == 0)
            hit = hit | due
            i = i + jnp.where(due, m * p.cpm + j, 0)

        @pl.when(hit)
        def _():
            act(i)

    def service(seg):
        for d, role in ((0, role_a), (1, role_b)):
            def sums(i, d=d, role=role):
                mine = chain(d, i)[0]
                arrived = stage.at[d, lax.rem(i, 2)]

                @pl.when(role > 0)
                def _():
                    st_copy(d, i).wait()

                @pl.when((role > 0) & (role < 3))
                def _():
                    mine[...] = mine[...] + arrived[...]

                @pl.when(role < 3)
                def _():
                    rs_copy(d, i).start()

                @pl.when(role == 3)
                def _():
                    k = lax.rem(i, p.cpm)

                    @pl.when(i >= p.cpm)
                    def _():
                        yl_copy(d, i - p.cpm).wait()
                        ag_copy(d, i - p.cpm, yst.at[d, k]).wait_send()

                    yst[d, k] = (mine[...] + arrived[...]).astype(jnp.bfloat16)
                    yl_copy(d, i).start()
                    ag_copy(d, i, yst.at[d, k]).start()

            when_due(seg, role, p.sums, 0, sums)

        for d, role in ((0, role_a), (1, role_b)):
            def rows(i, d=d, role=role):
                @pl.when(role < 3)
                def _():
                    ag_copy(d, i).wait_recv()

                @pl.when((role < 3) & (role > 0))
                def _():
                    ag_copy(d, i).start()

            when_due(seg, 2 - role, p.rows, 0, rows)

        for d, role in ((0, role_a), (1, role_b)):
            def fetch(i, d=d, role=role):
                @pl.when(role > 0)
                def _():
                    rs_copy(d, i).wait_recv()
                    st_copy(d, i).start()

            when_due(seg, role, p.sums, 1, fetch)

    row_id = lax.broadcasted_iota(jnp.int32, (p.mr, 1), 0)
    mine_a = jnp.where(tp == 0, 1, 0)
    mine_b = jnp.where(tp == 3, 1, 0)
    take_x = jnp.where(row_id < p.half, mine_a, mine_b).astype(jnp.float32)

    def xb_copy(m):
        return pltpu.make_async_copy(x.at[pl.ds(pl.multiple_of(m * p.mr, p.mr), p.mr)], xb, b_sem.at[5])

    def first_q(t, _):
        q_tile(t)

        @pl.when(t == max(0, p.nq - 3))
        def _():
            for n in range(p.nt):
                wo_copy(n).start()

        return 0

    lax.fori_loop(0, p.nq, first_q, 0)

    def segment(seg, _):
        m = seg // p.nseg
        s = lax.rem(seg, p.nseg)
        busy = m < p.nm

        @pl.when(busy & (s < p.s_near))
        def _():
            @pl.when(s == 0)
            def _():
                xb_copy(m).start()

            own_segment(m, s)

        @pl.when(seg == p.s_near)
        def _():
            for c in cache_copies(across, partner, 1):
                c.wait_recv()
            for c in cache_copies(across, partner, 2):
                c.start()
            for k in (0, 2):
                for c in cache_copies(cp, partner, k):
                    c.wait_recv()

            @pl.when(lax.rem(cp, 2) == 1)
            def _():
                for c in new_copies(pl.multiple_of(p.tok * cp, p.tok), p.tok, partner, 0):
                    c.wait_recv()

        @pl.when(busy & (s >= p.s_near) & (s < p.s_far))
        def _():
            block_segment(m, s - p.s_near, near, lambda b: b * p.tok * cp)

        @pl.when((seg == p.s_far) & (cp >= 2))
        def _():
            got = pl.multiple_of(p.tok * (cp - 1), p.tok)
            for c in new_copies(got, p.tok, partner, 1):
                c.wait_recv()
            for c in new_copies(got, p.tok, partner, 2):
                c.start()
            for c in new_copies(got, p.tok, partner, 2):
                c.wait_recv()

        @pl.when(busy & (s >= p.s_far) & (s < p.s_fin) & (far > 0))
        def _():
            block_segment(m, s - p.s_far, far, lambda b: (1 + b) * p.tok)

        @pl.when(busy & (s == p.s_fin))
        def _():
            def finish(i, _):
                inv = 1.0 / jnp.sum(l_s[i], axis=0, keepdims=True)
                v = o_t[i] * inv
                for k in range(QUAD):
                    o[:, pl.ds(pl.multiple_of((i * QUAD + k) * HEAD, HEAD), HEAD)] = v[:, k * p.mr:(k + 1) * p.mr].T.astype(jnp.bfloat16)
                return reset(i, 0)

            lax.fori_loop(0, p.nq, finish, 0)

        @pl.when(busy & (s >= p.s_out) & (s < p.s_q))
        def _():
            n = s - p.s_out

            @pl.when(n == 0)
            def _():
                xb_copy(m).wait()

            @pl.when((n == 0) & (m >= p.owns))
            def _():
                for d, role in ((0, role_a), (1, role_b)):
                    @pl.when(role < 3)
                    def _():
                        for j in range(p.cpm):
                            rs_copy(d, (m - p.owns) * p.cpm + j).wait_send()

            @pl.when(m == 0)
            def _():
                wo_copy(n).wait()

            a = jnp.dot(o[...], wo[n], preferred_element_type=jnp.float32)
            a = a + xb[:, pl.ds(pl.multiple_of(n * p.wcols, HEAD), p.wcols)].astype(jnp.float32) * take_x
            own[lax.rem(m, p.owns), n // p.per, :, pl.ds(pl.multiple_of(lax.rem(n, p.per) * p.wcols, HEAD), p.wcols)] = a

        @pl.when((m // 2 + 1 < p.np) & (s >= p.s_q))
        def _():
            q_tile((m // 2 + 1) * p.nq + lax.rem(m, 2) * p.hp + s - p.s_q)

        service(seg)
        return 0

    lax.fori_loop(0, p.total, segment, 0)

    for d, role in ((0, role_a), (1, role_b)):
        @pl.when(role < 3)
        def _():
            def last_sums(i, _):
                rs_copy(d, i).wait_send()
                return 0
            lax.fori_loop((p.nm - p.owns) * p.cpm, p.chunks, last_sums, 0)

        @pl.when((role > 0) & (role < 3))
        def _():
            def last_rows(i, _):
                ag_copy(d, i).wait_send()
                return 0
            lax.fori_loop(0, p.chunks, last_rows, 0)

        @pl.when(role == 3)
        def _():
            for k in range(p.cpm):
                i = p.chunks - p.cpm + k
                yl_copy(d, i).wait()
                ag_copy(d, i, yst.at[d, k]).wait_send()

    for c in out_copies():
        c.wait()
    for k in (0, 1):
        for c in cache_copies(cp, partner, k):
            c.wait_send()
    for c in cache_copies(across, partner, 2):
        c.wait_send()

    @pl.when(cp < 2)
    def _():
        for c in new_copies(new0, p.tok, across, 1):
            c.wait_send()

    @pl.when(lax.rem(cp, 2) == 0)
    def _():
        for c in new_copies(new0, p.tok, partner, 0):
            c.wait_send()

    @pl.when(cp >= 2)
    def _():
        for c in new_copies(pl.multiple_of(p.tok * (cp - 1), p.tok), p.tok, partner, 2):
            c.wait_send()


def build(p):
    def local_step(x, k_cache, v_cache, rope_table, norm_gain, w_qkv, b_qkv, w_out):
        small = jnp.concatenate([b_qkv, norm_gain]).astype(jnp.float32).reshape(1, -1)
        cached = jnp.stack([k_cache, v_cache]).transpose(0, 2, 1, 3)
        anyspace = pl.BlockSpec(memory_space=pl.ANY)
        vmem = pl.BlockSpec(memory_space=pltpu.VMEM)
        bf, f32 = jnp.bfloat16, jnp.float32
        dma = pltpu.SemaphoreType.DMA
        kvw = p.kv * HEAD
        y, kn, vn, _ = pl.pallas_call(
            functools.partial(kernel, p),
            name='block',
            out_shape=(jax.ShapeDtypeStruct((p.tok, p.dim), bf), jax.ShapeDtypeStruct((p.tok, kvw), bf), jax.ShapeDtypeStruct((p.tok, kvw), bf),
                       jax.ShapeDtypeStruct((2, p.chunks, p.half, p.cc), f32)),
            in_specs=[anyspace, anyspace, anyspace, vmem, anyspace, anyspace],
            out_specs=(anyspace, anyspace, anyspace, anyspace),
            scratch_shapes=[
                pltpu.VMEM((p.tok, p.dim), bf),
                pltpu.VMEM((p.kv, p.keys, HEAD), bf),
                pltpu.VMEM((p.kv, HEAD, p.keys), bf),
                pltpu.VMEM((p.tok, 64), f32),
                pltpu.VMEM((4, p.nq, p.n, HEAD), bf),
                pltpu.VMEM((p.nq, HEAD, p.n), f32),
                pltpu.VMEM((p.mr, p.heads * HEAD), bf),
                pltpu.VMEM((p.kt, p.n), f32),
                pltpu.VMEM((p.kt, p.n), f32),
                pltpu.VMEM((p.kt, p.n), bf),
                pltpu.VMEM((8, p.n), f32),
                pltpu.VMEM((8, p.n), f32),
                pltpu.VMEM((p.nq, 8, p.n), f32),
                pltpu.VMEM((p.nq, 8, p.n), f32),
                pltpu.VMEM((p.owns, p.cpm, p.mr, p.cc), f32),
                pltpu.VMEM((2, 2, p.half, p.cc), f32),
                pltpu.VMEM((2, p.cpm, p.half, p.cc), bf),
                pltpu.VMEM((p.mr, p.dim), bf),
                pltpu.VMEM((2, p.dim, p.wcols), bf),
                pltpu.VMEM((p.nt, p.heads * HEAD, p.wcols), bf),
                pltpu.VMEM((p.kv, p.tok, HEAD), bf),
                dma((4,)), dma((2,)), dma((p.nt,)), dma((6,)), dma((2 * p.kv,)),
                dma((3, 2)), dma((3, 2)), dma((3, 2)), dma((3, 2)),
                dma((2, p.chunks)), dma((2, p.chunks)), dma((2, 2)), dma((2, p.chunks)), dma((2, p.chunks)), dma((2, p.cpm)),
            ],
            compiler_params=pltpu.CompilerParams(collective_id=0, has_side_effects=True, vmem_limit_bytes=67_000_000),
        )(x, cached, rope_table, small, w_qkv, w_out)
        shape = (p.tok, p.kv, HEAD)
        return y, kn.reshape(shape), vn.reshape(shape)

    return local_step


def solution(mesh):
    row_spec = P(('dp', 'cp'), None)
    cache_spec = P(('dp', 'cp'), 'tp', None)
    p = Plan(tok=1024, dim=4096, kv=2, group=12, cache=256, nm=8, kt=512)
    p.table([[11, 19, 22, 24], [21, 25, 28, 32], [26, 29, 37, 43], [37, 43, 45, 47]],
            [[45, 48, 53, 59], [48, 56, 65, 66], [64, 69, 71, 74]])
    return jax.shard_map(build(p), mesh=mesh, in_specs=(row_spec, cache_spec, cache_spec, row_spec, P(None), P(None, 'tp'), P('tp'), P('tp', None)),
                         out_specs=(row_spec, cache_spec, cache_spec), check_vma=False)
```

time: 440 us -> 433 us (0.984)
    unnamed x3 -> x2, local copies, waits for them, and re-layouts: 11.1 us -> 9.83 us
where the time goes in v2:
time: 433 us; the launch traced here: 431 us
  Pallas kernels  413 us (95%)
  local copies, waits for them, and re-layouts  16.2 us (4%)
    pallas_call x1, Pallas kernels, local_step(): pl.pallas_call(functools.partial(kernel, p), name='block', out_shape=(jax...  413 us
    unnamed x2, local copies, waits for them, and re-layouts  9.83 us

profile of v2, /device:TPU:5, one launch (start us, length us, event | category | flops | bytes accessed | tf_op | source)
XLA Modules:
  0.0 431.3 jit_solution(9710364727391778106)
XLA Ops:
  0.6 0.7 concatenate.14
  1.3 0.7 concatenate.15
  2.1 0.6 maximum_convert_fusion.small
  2.7 1.0 copy_bitcast_fusion
  3.7 0.7 maximum_bitcast_fusion.cache_in
  4.4 1.9 copy.13.rope_in
  6.4 413.1 %block.1 = (bf16[1024,4096]{1,0:T(8,128)(2,1)}, bf16[1024,256]{1,0:T(8,128)(2,1)}, bf16[1024,256]{1,0:T(8,128)(2,1)}, f32[2,32,64,1024]{3,2,1,0:T(8,128)}) custom-call(bf16[1024,4096]{1,0:T(8,128)(2,1)} %x.1, bf16[2,2,256,128]{3,2,1,0:T(8,128)(2,1)} %maximum_bitcast_fusion.cache_in, f32[1024,64]{1,0:T(8,128)} %copy.13.rope_in, ...), custom_call_target="tpu_custom_call" | custom-call | tf_op jit(solution)/shard_map/block/pallas_call | solution.py:588
  419.5 2.0 reshape.42
  421.4 2.0 reshape.43
  423.4 7.9 %copy.17 = bf16[1024,4096]{1,0:T(8,128)(2,1)} copy(bf16[1024,4096]{1,0:T(8,128)(2,1)} %get-tuple-element.14) | data formatting | bytes 16777216

commit v3 on v2

--- a/solution.py
+++ b/solution.py
@@ -20,27 +20,29 @@
         self.tok, self.dim, self.kv, self.group, self.cache = tok, dim, kv, group, cache
         self.nm = nm
         self.mr = tok // nm
-        self.np = nm // 2
         self.kt = kt
-        self.nq = kv * group // QUAD
+        self.heads = kv * group
+        self.nd = self.heads // 2
+        self.dpg = group // 2
+        self.n = 2 * self.mr
+        self.keys = tok * 5
+        self.wcols = QUAD * HEAD
+        self.nq = self.heads // QUAD
         self.qpg = group // QUAD
-        self.hp = self.nq // 2
-        self.n = QUAD * self.mr
-        self.keys = tok * 5
-        self.heads = kv * group
-        self.wcols = QUAD * HEAD
+        self.hq = self.nq // 2
         self.nt = dim // self.wcols
         self.cpm = 4
         self.per = self.nt // self.cpm
         self.cc = dim // self.cpm
         self.half = self.mr // 2
         self.owns = 2
-        self.s_near = self.hp
-        self.s_far = self.s_near + self.hp
-        self.s_fin = self.s_far + self.hp
+        self.look = 3
+        self.wt = self.nq * (2 + nm // 2 - 1)
+        self.s_blk = 2
+        self.s_fin = self.s_blk + 4
         self.s_out = self.s_fin + 1
         self.s_q = self.s_out + self.nt
-        self.nseg = self.s_q + self.hp
+        self.nseg = self.s_q + self.hq
         self.chunks = nm * self.cpm
         self.table([[self.s_out + self.per * (j + 1) - 1 + 3 * r for j in range(self.cpm)] for r in range(4)],
                    [[self.s_out + self.per * (j + 1) - 1 + 12 + 3 * r for j in range(self.cpm)] for r in range(3)])
@@ -50,7 +52,7 @@
         self.total = self.nseg * (self.nm - 1) + max(max(r) for r in sums + rows) + 1
 
 def kernel(p, x, cache_in, rope_in, small, wqkv, wout, y, kn, vn, land,
-           h, ka, vt, rope, q, o_t, o, s_a, s_b, p_s, mx_a, mx_b, m_s, l_s, own, stage, yst, xb, w, wo, vb,
+           h, ka, vt, rope, q, o_t, o, s_t, mx_t, m_s, l_s, own, stage, yst, xb, w, wo, vb,
            x_sem, w_sem, wo_sem, b_sem, out_sem, cs_send, cs_recv, kv_send, kv_recv,
            rs_send, rs_recv, st_sem, ag_send, ag_recv, yl_sem):
     tp = lax.axis_index('tp')
@@ -90,9 +92,6 @@
     vc_copy.start()
     rope_copy = pltpu.make_async_copy(rope_in, rope, b_sem.at[2])
     rope_copy.start()
-    for r in range(1, 4):
-        x_copy(r).start()
-    wq_copy(0).start()
 
     barrier = pltpu.get_barrier_semaphore()
     for k in range(1, 4):
@@ -154,8 +153,12 @@
     rope_copy.wait()
     for g in range(p.kv):
         wkv_copy(g).wait()
-    nsub = max(1, rows4 // 64)
+    for r in range(1, 4):
+        x_copy(r).start()
+    wq_copy(0).start()
+    nsub = max(1, rows4 // 128)
     sub = rows4 // nsub
+    wide = 512
 
     def kv_step(r, _):
         x_copy(r).wait()
@@ -166,9 +169,16 @@
 
         def norm(b, _):
             rows = pl.ds(pl.multiple_of(r * rows4 + b * sub, sub), sub)
-            v = h[rows, :].astype(jnp.float32)
-            inv = lax.rsqrt(jnp.mean(v * v, axis=1, keepdims=True) + EPS)
-            h[rows, :] = (v * inv * small[0:1, goff:goff + p.dim]).astype(jnp.bfloat16)
+            total = None
+            for c in range(0, p.dim, wide):
+                v = h[rows, c:c + wide].astype(jnp.float32)
+                v = v * v
+                for k in range(0, wide, HEAD):
+                    total = v[:, k:k + HEAD] if total is None else total + v[:, k:k + HEAD]
+            inv = lax.rsqrt(jnp.sum(total, axis=1, keepdims=True) * (1.0 / p.dim) + EPS)
+            for c in range(0, p.dim, wide):
+                v = h[rows, c:c + wide].astype(jnp.float32)
+                h[rows, c:c + wide] = (v * inv * small[0:1, goff + c:goff + c + wide]).astype(jnp.bfloat16)
             return 0
 
         lax.fori_loop(0, nsub, norm, 0)
@@ -206,114 +216,98 @@
         o_t[i] = jnp.zeros((HEAD, p.n), jnp.float32)
         return 0
 
-    lax.fori_loop(0, p.nq, reset, 0)
-
-    def q_tile(t):
-        pair = t // p.nq
+    lax.fori_loop(0, p.nd, reset, 0)
+
+    def q_tile(t, first, count):
         j = lax.rem(t, p.nq)
-        rows = pl.ds(pl.multiple_of(pair * 2 * p.mr, 2 * p.mr), 2 * p.mr)
+        rows = pl.ds(pl.multiple_of(first * p.mr, p.mr), count * p.mr)
         wq_copy(t).wait()
         a = jnp.dot(h[rows, :], w[lax.rem(t, 2)], preferred_element_type=jnp.float32)
         a = a + small[0:1, pl.ds(pl.multiple_of(wq_col(j), HEAD), p.wcols)]
-        c, s = angles(rows, 2 * p.mr)
+        c, s = angles(rows, count * p.mr)
         for k in range(QUAD):
             b = rotate(a[:, k * HEAD:(k + 1) * HEAD], c, s).astype(jnp.bfloat16)
-            for u in range(2):
-                q[2 * lax.rem(pair, 2) + u, j, k * p.mr:(k + 1) * p.mr, :] = b[u * p.mr:(u + 1) * p.mr, :]
-
-        @pl.when(t + 2 < p.np * p.nq)
+            for u in range(count):
+                q[lax.rem(first + u, 4), 2 * j + k // 2, (k % 2) * p.mr:(k % 2 + 1) * p.mr, :] = b[u * p.mr:(u + 1) * p.mr, :]
+
+        @pl.when(t + 2 < p.wt)
         def _():
             wq_copy(t + 2).start()
 
-    sb = min(256, p.kt)
-    ss = min(128, p.kt)
-    pk = min(256, p.kt)
-
-    def scores(qs, hq, off, kk, s_ref, mx, bound):
-        g = hq // p.qpg
-        s = lax.dot_general(ka[g, pl.ds(pl.multiple_of(off + kk, sb), sb), :], q[qs, hq], (((1,), (1,)), ((), ())),
+    part_rows = min(256, p.kt)
+    row_of = lax.rem(lax.broadcasted_iota(jnp.int32, (p.kt, p.n), 1), p.mr) - lax.broadcasted_iota(jnp.int32, (p.kt, p.n), 0)
+
+    def scores(qs, pair, off, k, bound):
+        g = pair // p.dpg
+        s = lax.dot_general(ka[g, pl.ds(pl.multiple_of(off, p.kt), p.kt), :], q[qs, pair], (((1,), (1,)), ((), ())),
                             preferred_element_type=jnp.float32) * scale
         if bound is not None:
-            row = lax.rem(lax.broadcasted_iota(jnp.int32, (sb, p.n), 1), p.mr)
-            key = lax.broadcasted_iota(jnp.int32, (sb, p.n), 0)
-            s = jnp.where(row - key >= kk - bound, s, LOW)
-        s_ref[kk:kk + sb, :] = s
-        top = jnp.max(s.reshape(sb // 8, 8, p.n), axis=0)
-        return top if mx is None else jnp.maximum(mx, top)
-
-    def all_scores(qs, hq, off, s_ref, mx_ref, bound):
-        mx = None
-        for kk in range(0, p.kt, sb):
-            mx = scores(qs, hq, off, kk, s_ref, mx, bound)
-        mx_ref[...] = mx
-
-    def tile(qs, hq, off, s_ref, mx_ref, hq_n, off_n, s_next, mx_next, bound_n):
-        g = hq // p.qpg
-        m_old = m_s[hq, 0:1, :]
-        m_new = jnp.maximum(m_old, jnp.max(mx_ref[...], axis=0, keepdims=True))
+            s = jnp.where(row_of >= -bound, s, LOW)
+        s_t[k] = s
+        mx_t[k] = jnp.max(s.reshape(p.kt // 8, 8, p.n), axis=0)
+
+    def weigh(pair, off, k):
+        g = pair // p.dpg
+        m_old = m_s[pair, 0:1, :]
+        m_new = jnp.maximum(m_old, jnp.max(mx_t[k], axis=0, keepdims=True))
         alpha = jnp.exp2(m_old - m_new)
-        m_s[hq, 0:1, :] = m_new
-        mx = acc = out = None
-        for kk in range(0, p.kt, pk):
-            for k2 in range(kk, kk + pk, sb):
-                mx = scores(qs, hq_n, off_n, k2, s_next, mx, bound_n)
-            for k2 in range(kk, kk + pk, ss):
-                e = jnp.exp2(s_ref[k2:k2 + ss, :] - m_new)
-                part = jnp.sum(e.reshape(ss // 8, 8, p.n), axis=0)
-                acc = part if acc is None else acc + part
-                p_s[k2:k2 + ss, :] = e.astype(jnp.bfloat16)
-            d = jnp.dot(vt[g, :, pl.ds(pl.multiple_of(off + kk, pk), pk)], p_s[kk:kk + pk, :], preferred_element_type=jnp.float32)
-            out = d if out is None else out + d
-        mx_next[...] = mx
-        l_s[hq] = l_s[hq] * alpha + acc
-        o_t[hq] = o_t[hq] * alpha + out
-
-    def own_segment(u, i):
+        m_s[pair, 0:1, :] = m_new
+        acc = None
+        es = []
+        for r in range(0, p.kt, part_rows):
+            e = jnp.exp2(s_t[k, r:r + part_rows, :] - m_new)
+            part = jnp.sum(e.reshape(part_rows // 8, 8, p.n), axis=0)
+            acc = part if acc is None else acc + part
+            es.append(e.astype(jnp.bfloat16))
+        d = jnp.dot(vt[g, :, pl.ds(pl.multiple_of(off, p.kt), p.kt)], jnp.concatenate(es, axis=0), preferred_element_type=jnp.float32)
+        l_s[pair] = l_s[pair] * alpha + acc
+        o_t[pair] = o_t[pair] * alpha + d
+
+    anything = 1 << 20
+    slots = p.look + 1
+
+    def own_at(j):
+        return new0 + j * p.kt
+
+    def own_segment(u, j, tiles):
         qs = lax.rem(u, 4)
-        tiles = (u * p.mr + p.mr + p.kt - 1) // p.kt
-        h0 = 2 * i
-
-        def bound(j):
-            return u * p.mr - j * p.kt
-
-        @pl.when(i == 0)
-        def _():
-            all_scores(qs, 0, new0, s_a, mx_a, bound(0))
-
-        def step(j, _):
-            more = j + 1 < tiles
-            hn = jnp.where(more, h0, jnp.minimum(h0 + 2, p.nq - 2))
-            jn = jnp.where(more, j + 1, 0)
-            off = new0 + j * p.kt
-            tile(qs, h0, off, s_a, mx_a, h0 + 1, off, s_b, mx_b, bound(j))
-            tile(qs, h0 + 1, off, s_b, mx_b, hn, new0 + jn * p.kt, s_a, mx_a, bound(jn))
-            return 0
-
-        lax.fori_loop(0, tiles, step, 0)
-
-    def block_segment(u, i, count, offset):
+        bound = u * p.mr - j * p.kt
+        more = j + 1 < tiles
+
+        @pl.when(j == 0)
+        def _():
+            for i in range(p.look):
+                scores(qs, i, new0, i, u * p.mr)
+
+        for i in range(p.nd):
+            n = i + p.look
+            if n < p.nd:
+                scores(qs, n, own_at(j), n % slots, bound)
+            else:
+                n -= p.nd
+                scores(qs, jnp.where(more, n, n // 2), jnp.where(more, own_at(j + 1), (n % 2) * p.kt), (n + p.nd) % slots,
+                       jnp.where(more, bound - p.kt, anything))
+            weigh(i, own_at(j), i % slots)
+
+    def block_at(b):
+        return jnp.where(b == 0, 0, p.tok * (1 + jnp.where(lax.rem(cp, 2) == 1, cp - b, b - 1)))
+
+    def block_segment(u, b, count):
         qs = lax.rem(u, 4)
-        h0 = 2 * i
-
-        @pl.when(i == 0)
-        def _():
-            all_scores(qs, 0, offset(0), s_a, mx_a, None)
-
-        def step(b, _):
-            off = offset(b)
-            more = b + 1 < count
-            hn = jnp.where(more, h0, jnp.minimum(h0 + 2, p.nq - 2))
-            on = offset(jnp.where(more, b + 1, 0))
-            tile(qs, h0, off, s_a, mx_a, h0, off + p.kt, s_b, mx_b, None)
-            tile(qs, h0, off + p.kt, s_b, mx_b, h0 + 1, off, s_a, mx_a, None)
-            tile(qs, h0 + 1, off, s_a, mx_a, h0 + 1, off + p.kt, s_b, mx_b, None)
-            tile(qs, h0 + 1, off + p.kt, s_b, mx_b, hn, on, s_a, mx_a, None)
-            return 0
-
-        lax.fori_loop(0, count, step, 0)
-
-    near = 1 + lax.rem(cp, 2)
-    far = 2 * (cp // 2)
+        at = block_at(b)
+        following = jnp.where((u > 0) & (b + 1 < count), block_at(b + 1), 0)
+
+        @pl.when((u == 0) & (b > 0))
+        def _():
+            for i in range(p.look):
+                scores(qs, i // 2, at + (i % 2) * p.kt, i, None)
+
+        for i in range(2 * p.nd):
+            n = i + p.look
+            scores(qs, (n // 2) % p.nd, (at if n < 2 * p.nd else following) + (n % 2) * p.kt, n % slots, None)
+            weigh(i // 2, at + (i % 2) * p.kt, i % slots)
+
+    blocks = 1 + cp
 
     role_a = 3 - tp
     role_b = tp
@@ -420,16 +414,15 @@
 
             when_due(seg, role, p.sums, 1, fetch)
 
-    row_id = lax.broadcasted_iota(jnp.int32, (p.mr, 1), 0)
-    mine_a = jnp.where(tp == 0, 1, 0)
-    mine_b = jnp.where(tp == 3, 1, 0)
-    take_x = jnp.where(row_id < p.half, mine_a, mine_b).astype(jnp.float32)
+    take_a = jnp.where(tp == 0, 1, 0).astype(jnp.float32)
+    take_b = jnp.where(tp == 3, 1, 0).astype(jnp.float32)
+    x_half = jnp.where(tp == 3, p.half, 0)
 
     def xb_copy(m):
-        return pltpu.make_async_copy(x.at[pl.ds(pl.multiple_of(m * p.mr, p.mr), p.mr)], xb, b_sem.at[5])
+        return pltpu.make_async_copy(x.at[pl.ds(pl.multiple_of(m * p.mr + x_half, p.half), p.half)], xb, b_sem.at[5])
 
     def first_q(t, _):
-        q_tile(t)
+        q_tile(t, 0, 1)
 
         @pl.when(t == max(0, p.nq - 3))
         def _():
@@ -439,63 +432,61 @@
         return 0
 
     lax.fori_loop(0, p.nq, first_q, 0)
+
+    for c in cache_copies(across, partner, 1):
+        c.wait_recv()
+    for c in cache_copies(across, partner, 2):
+        c.start()
+    for k in (0, 2):
+        for c in cache_copies(cp, partner, k):
+            c.wait_recv()
 
     def segment(seg, _):
         m = seg // p.nseg
         s = lax.rem(seg, p.nseg)
         busy = m < p.nm
-
-        @pl.when(busy & (s < p.s_near))
+        tiles = (m * p.mr + p.mr + p.kt - 1) // p.kt
+
+        @pl.when(busy & (s < tiles) & (s < p.s_blk))
         def _():
             @pl.when(s == 0)
             def _():
                 xb_copy(m).start()
 
-            own_segment(m, s)
-
-        @pl.when(seg == p.s_near)
-        def _():
-            for c in cache_copies(across, partner, 1):
+            own_segment(m, s, tiles)
+
+        @pl.when((seg == p.s_blk + 1) & (lax.rem(cp, 2) == 1))
+        def _():
+            for c in new_copies(pl.multiple_of(p.tok * cp, p.tok), p.tok, partner, 0):
                 c.wait_recv()
-            for c in cache_copies(across, partner, 2):
+
+        @pl.when((cp >= 2) & (seg == p.s_blk + cp - 1))
+        def _():
+            direct = pl.multiple_of(p.tok * (cp - 1), p.tok)
+            for c in new_copies(direct, p.tok, partner, 1):
+                c.wait_recv()
+            for c in new_copies(direct, p.tok, partner, 2):
                 c.start()
-            for k in (0, 2):
-                for c in cache_copies(cp, partner, k):
-                    c.wait_recv()
-
-            @pl.when(lax.rem(cp, 2) == 1)
-            def _():
-                for c in new_copies(pl.multiple_of(p.tok * cp, p.tok), p.tok, partner, 0):
-                    c.wait_recv()
-
-        @pl.when(busy & (s >= p.s_near) & (s < p.s_far))
-        def _():
-            block_segment(m, s - p.s_near, near, lambda b: b * p.tok * cp)
-
-        @pl.when((seg == p.s_far) & (cp >= 2))
-        def _():
-            got = pl.multiple_of(p.tok * (cp - 1), p.tok)
-            for c in new_copies(got, p.tok, partner, 1):
+
+        @pl.when((cp >= 2) & (seg == p.s_blk + cp))
+        def _():
+            for c in new_copies(pl.multiple_of(p.tok * (cp - 1), p.tok), p.tok, partner, 2):
                 c.wait_recv()
-            for c in new_copies(got, p.tok, partner, 2):
-                c.start()
-            for c in new_copies(got, p.tok, partner, 2):
-                c.wait_recv()
-
-        @pl.when(busy & (s >= p.s_far) & (s < p.s_fin) & (far > 0))
-        def _():
-            block_segment(m, s - p.s_far, far, lambda b: (1 + b) * p.tok)
+
+        @pl.when(busy & (s >= p.s_blk) & (s < p.s_blk + blocks))
+        def _():
+            block_segment(m, s - p.s_blk, blocks)
 
         @pl.when(busy & (s == p.s_fin))
         def _():
             def finish(i, _):
                 inv = 1.0 / jnp.sum(l_s[i], axis=0, keepdims=True)
                 v = o_t[i] * inv
-                for k in range(QUAD):
-                    o[:, pl.ds(pl.multiple_of((i * QUAD + k) * HEAD, HEAD), HEAD)] = v[:, k * p.mr:(k + 1) * p.mr].T.astype(jnp.bfloat16)
+                for k in range(2):
+                    o[:, pl.ds(pl.multiple_of((i * 2 + k) * HEAD, HEAD), HEAD)] = v[:, k * p.mr:(k + 1) * p.mr].T.astype(jnp.bfloat16)
                 return reset(i, 0)
 
-            lax.fori_loop(0, p.nq, finish, 0)
+            lax.fori_loop(0, p.nd, finish, 0)
 
         @pl.when(busy & (s >= p.s_out) & (s < p.s_q))
         def _():
@@ -518,12 +509,24 @@
                 wo_copy(n).wait()
 
             a = jnp.dot(o[...], wo[n], preferred_element_type=jnp.float32)
-            a = a + xb[:, pl.ds(pl.multiple_of(n * p.wcols, HEAD), p.wcols)].astype(jnp.float32) * take_x
-            own[lax.rem(m, p.owns), n // p.per, :, pl.ds(pl.multiple_of(lax.rem(n, p.per) * p.wcols, HEAD), p.wcols)] = a
-
-        @pl.when((m // 2 + 1 < p.np) & (s >= p.s_q))
-        def _():
-            q_tile((m // 2 + 1) * p.nq + lax.rem(m, 2) * p.hp + s - p.s_q)
+            r = xb[:, pl.ds(pl.multiple_of(n * p.wcols, HEAD), p.wcols)].astype(jnp.float32)
+            cols = pl.ds(pl.multiple_of(lax.rem(n, p.per) * p.wcols, HEAD), p.wcols)
+            own[lax.rem(m, p.owns), n // p.per, 0:p.half, cols] = a[0:p.half] + r * take_a
+            own[lax.rem(m, p.owns), n // p.per, p.half:p.mr, cols] = a[p.half:p.mr] + r * take_b
+
+        @pl.when((m == 0) & (s >= p.s_q))
+        def _():
+            for k in range(2):
+                q_tile(p.nq + 2 * (s - p.s_q) + k, 1, 1)
+
+        @pl.when((m == 1) & (s >= p.s_q))
+        def _():
+            for k in range(2):
+                q_tile(2 * p.nq + 2 * (s - p.s_q) + k, 2, 2)
+
+        @pl.when((m >= 2) & (m < p.nm - 2) & (s >= p.s_q))
+        def _():
+            q_tile(3 * p.nq + (m - 2) * p.hq + s - p.s_q, m - lax.rem(m, 2) + 2, 2)
 
         service(seg)
         return 0
@@ -597,20 +600,17 @@
                 pltpu.VMEM((p.kv, p.keys, HEAD), bf),
                 pltpu.VMEM((p.kv, HEAD, p.keys), bf),
                 pltpu.VMEM((p.tok, 64), f32),
-                pltpu.VMEM((4, p.nq, p.n, HEAD), bf),
-                pltpu.VMEM((p.nq, HEAD, p.n), f32),
+                pltpu.VMEM((4, p.nd, p.n, HEAD), bf),
+                pltpu.VMEM((p.nd, HEAD, p.n), f32),
                 pltpu.VMEM((p.mr, p.heads * HEAD), bf),
-                pltpu.VMEM((p.kt, p.n), f32),
-                pltpu.VMEM((p.kt, p.n), f32),
-                pltpu.VMEM((p.kt, p.n), bf),
-                pltpu.VMEM((8, p.n), f32),
-                pltpu.VMEM((8, p.n), f32),
-                pltpu.VMEM((p.nq, 8, p.n), f32),
-                pltpu.VMEM((p.nq, 8, p.n), f32),
+                pltpu.VMEM((p.look + 1, p.kt, p.n), f32),
+                pltpu.VMEM((p.look + 1, 8, p.n), f32),
+                pltpu.VMEM((p.nd, 8, p.n), f32),
+                pltpu.VMEM((p.nd, 8, p.n), f32),
                 pltpu.VMEM((p.owns, p.cpm, p.mr, p.cc), f32),
                 pltpu.VMEM((2, 2, p.half, p.cc), f32),
                 pltpu.VMEM((2, p.cpm, p.half, p.cc), bf),
-                pltpu.VMEM((p.mr, p.dim), bf),
+                pltpu.VMEM((p.half, p.dim), bf),
                 pltpu.VMEM((2, p.dim, p.wcols), bf),
                 pltpu.VMEM((p.nt, p.heads * HEAD, p.wcols), bf),
                 pltpu.VMEM((p.kv, p.tok, HEAD), bf),
@@ -630,7 +630,7 @@
     row_spec = P(('dp', 'cp'), None)
     cache_spec = P(('dp', 'cp'), 'tp', None)
     p = Plan(tok=1024, dim=4096, kv=2, group=12, cache=256, nm=8, kt=512)
-    p.table([[11, 19, 22, 24], [21, 25, 28, 32], [26, 29, 37, 43], [37, 43, 45, 47]],
-            [[45, 48, 53, 59], [48, 56, 65, 66], [64, 69, 71, 74]])
+    p.table([[8, 14, 16, 19], [15, 17, 20, 22], [19, 22, 27, 33], [31, 35, 38, 40]],
+            [[36, 39, 41, 47], [39, 45, 51, 53], [54, 57, 59, 61]])
     return jax.shard_map(build(p), mesh=mesh, in_specs=(row_spec, cache_spec, cache_spec, row_spec, P(None), P(None, 'tp'), P('tp'), P('tp', None)),
                          out_specs=(row_spec, cache_spec, cache_spec), check_vma=False)

time: 433 us -> 374 us (0.86)
  Pallas kernels: 413 us -> 354 us
    pallas_call x1, Pallas kernels: 413 us -> 354 us  [local_step(): pl.pallas_call(functools.partial(kernel, p), name='block', out_shape=(jax...]
where the time goes in v3:
time: 374 us; the launch traced here: 372 us
  Pallas kernels  354 us (95%)
  local copies, waits for them, and re-layouts  16.2 us (4%)
    pallas_call x1, Pallas kernels, local_step(): pl.pallas_call(functools.partial(kernel, p), name='block', out_shape=(jax...  354 us
    unnamed x2, local copies, waits for them, and re-layouts  9.83 us

profile of v3, /device:TPU:5, one launch (start us, length us, event | category | flops | bytes accessed | tf_op | source)
XLA Modules:
  0.0 372.4 jit_solution(5592156277738628776)
XLA Ops:
  0.6 0.7 concatenate.14
  1.3 0.7 concatenate.15
  2.1 0.6 maximum_convert_fusion.small
  2.7 1.0 copy_bitcast_fusion
  3.7 0.7 maximum_bitcast_fusion.cache_in
  4.4 1.9 copy.13.rope_in
  6.4 354.2 %block.1 = (bf16[1024,4096]{1,0:T(8,128)(2,1)}, bf16[1024,256]{1,0:T(8,128)(2,1)}, bf16[1024,256]{1,0:T(8,128)(2,1)}, f32[2,32,64,1024]{3,2,1,0:T(8,128)}) custom-call(bf16[1024,4096]{1,0:T(8,128)(2,1)} %x.1, bf16[2,2,256,128]{3,2,1,0:T(8,128)(2,1)} %maximum_bitcast_fusion.cache_in, f32[1024,64]{1,0:T(8,128)} %copy.13.rope_in, ...), custom_call_target="tpu_custom_call" | custom-call | tf_op jit(solution)/shard_map/block/pallas_call | solution.py:591
  360.6 2.0 reshape.42
  362.6 2.0 reshape.43
  364.5 7.9 %copy.17 = bf16[1024,4096]{1,0:T(8,128)(2,1)} copy(bf16[1024,4096]{1,0:T(8,128)(2,1)} %get-tuple-element.14) | data formatting | bytes 16777216

commit v4 on v3

--- a/solution.py
+++ b/solution.py
@@ -36,8 +36,9 @@
         self.cc = dim // self.cpm
         self.half = self.mr // 2
         self.owns = 2
+        self.fin = math.gcd(self.nd, 3)
         self.look = 3
-        self.wt = self.nq * (2 + nm // 2 - 1)
+        self.wt = self.nq * (nm // 2)
         self.s_blk = 2
         self.s_fin = self.s_blk + 4
         self.s_out = self.s_fin + 1
@@ -51,8 +52,8 @@
         self.sums, self.rows = sums, rows
         self.total = self.nseg * (self.nm - 1) + max(max(r) for r in sums + rows) + 1
 
-def kernel(p, x, cache_in, rope_in, small, wqkv, wout, y, kn, vn, land,
-           h, ka, vt, rope, q, o_t, o, s_t, mx_t, m_s, l_s, own, stage, yst, xb, w, wo, vb,
+def kernel(p, x, k_in, v_in, rope_in, gain_in, bias_in, wqkv, wout, y, kn, vn, land,
+           h, ka, vt, rope_t, rope, b1, g1, small, cached, q, o_t, o, s_t, mx_t, m_s, l_s, own, stage, yst, xb, w, wo, kv_out,
            x_sem, w_sem, wo_sem, b_sem, out_sem, cs_send, cs_recv, kv_send, kv_recv,
            rs_send, rs_recv, st_sem, ag_send, ag_recv, yl_sem):
     tp = lax.axis_index('tp')
@@ -86,12 +87,11 @@
     x_copy(0).start()
     for g in range(p.kv):
         wkv_copy(g).start()
-    kc_copy = pltpu.make_async_copy(cache_in.at[0], ka.at[:, pl.ds(cp * p.cache, p.cache)], b_sem.at[3])
-    vc_copy = pltpu.make_async_copy(cache_in.at[1], vb.at[:, pl.ds(0, p.cache)], b_sem.at[4])
-    kc_copy.start()
-    vc_copy.start()
-    rope_copy = pltpu.make_async_copy(rope_in, rope, b_sem.at[2])
-    rope_copy.start()
+    little = [pltpu.make_async_copy(rope_in, rope_t, b_sem.at[2]), pltpu.make_async_copy(k_in, cached.at[0], b_sem.at[3]),
+              pltpu.make_async_copy(v_in, cached.at[1], b_sem.at[4]), pltpu.make_async_copy(bias_in, b1, b_sem.at[6]),
+              pltpu.make_async_copy(gain_in, g1, b_sem.at[7])]
+    for c in little:
+        c.start()
 
     barrier = pltpu.get_barrier_semaphore()
     for k in range(1, 4):
@@ -111,10 +111,15 @@
         return (pltpu.make_async_remote_copy(ks, ks, kv_send.at[k, 0], kv_recv.at[k, 0], device_id={'cp': peer}, device_id_type=MESH),
                 pltpu.make_async_remote_copy(vs, vs, kv_send.at[k, 1], kv_recv.at[k, 1], device_id={'cp': peer}, device_id_type=MESH))
 
-    vc_copy.wait()
+    for c in little:
+        c.wait()
+    here = pl.multiple_of(cp * p.cache, p.cache)
     for g in range(p.kv):
-        vt[g, :, pl.ds(pl.multiple_of(cp * p.cache, p.cache), p.cache)] = vb[g, 0:p.cache, :].astype(jnp.float32).T.astype(jnp.bfloat16)
-    kc_copy.wait()
+        ka[g, pl.ds(here, p.cache), :] = cached[0].astype(jnp.float32)[:, g, :].astype(jnp.bfloat16)
+        vt[g, :, pl.ds(here, p.cache)] = cached[1].astype(jnp.float32)[:, g, :].T.astype(jnp.bfloat16)
+    small[0:1, 0:goff] = b1[...].astype(jnp.float32).reshape(1, goff)
+    small[0:1, goff:goff + p.dim] = g1[...].astype(jnp.float32).reshape(1, p.dim)
+    rope[...] = rope_t[...].T
     pl.semaphore_wait(barrier, 6)
     for peer, k in ((across, 1), (partner, 0)):
         for c in cache_copies(cp, peer, k):
@@ -150,7 +155,6 @@
         swap = jnp.where(even, pltpu.roll(a, HEAD - 1, 1), pltpu.roll(a, 1, 1))
         return jnp.where(turned, a * c + swap * s, a)
 
-    rope_copy.wait()
     for g in range(p.kv):
         wkv_copy(g).wait()
     for r in range(1, 4):
@@ -160,52 +164,58 @@
     sub = rows4 // nsub
     wide = 512
 
-    def kv_step(r, _):
-        x_copy(r).wait()
-
-        @pl.when(r > 0)
-        def _():
-            send_new(r - 1)
-
-        def norm(b, _):
-            rows = pl.ds(pl.multiple_of(r * rows4 + b * sub, sub), sub)
-            total = None
-            for c in range(0, p.dim, wide):
-                v = h[rows, c:c + wide].astype(jnp.float32)
-                v = v * v
-                for k in range(0, wide, HEAD):
-                    total = v[:, k:k + HEAD] if total is None else total + v[:, k:k + HEAD]
-            inv = lax.rsqrt(jnp.sum(total, axis=1, keepdims=True) * (1.0 / p.dim) + EPS)
-            for c in range(0, p.dim, wide):
-                v = h[rows, c:c + wide].astype(jnp.float32)
-                h[rows, c:c + wide] = (v * inv * small[0:1, goff + c:goff + c + wide]).astype(jnp.bfloat16)
-            return 0
-
-        lax.fori_loop(0, nsub, norm, 0)
+    def norm(b):
+        rows = pl.ds(pl.multiple_of(b * sub, sub), sub)
+        total = None
+        for c in range(0, p.dim, wide):
+            v = h[rows, c:c + wide].astype(jnp.float32)
+            v = v * v
+            for k in range(0, wide, HEAD):
+                total = v[:, k:k + HEAD] if total is None else total + v[:, k:k + HEAD]
+        inv = lax.rsqrt(jnp.sum(total, axis=1, keepdims=True) * (1.0 / p.dim) + EPS)
+        for c in range(0, p.dim, wide):
+            v = h[rows, c:c + wide].astype(jnp.float32)
+            h[rows, c:c + wide] = (v * inv * small[0:1, goff + c:goff + c + wide]).astype(jnp.bfloat16)
+
+    def keys_values(r, ahead):
         rows = pl.ds(pl.multiple_of(r * rows4, rows4), rows4)
         at = pl.multiple_of(new0 + r * rows4, rows4)
         a = jnp.dot(h[rows, :], w[1], preferred_element_type=jnp.float32)
+        if ahead:
+            for b in range(nsub):
+                norm((r + 1) * nsub + b)
         c, s = angles(rows, rows4)
+        keys, vals = [], []
         for g in range(p.kv):
             col = g * (p.group + 2) * HEAD + p.group * HEAD
-            key = rotate(a[:, g * 2 * HEAD:g * 2 * HEAD + HEAD] + small[0:1, col:col + HEAD], c, s)
-            val = a[:, g * 2 * HEAD + HEAD:(g + 1) * 2 * HEAD] + small[0:1, col + HEAD:col + 2 * HEAD]
-            ka[g, pl.ds(at, rows4), :] = key.astype(jnp.bfloat16)
-            vb[g, rows, :] = val.astype(jnp.bfloat16)
-            vt[g, :, pl.ds(at, rows4)] = val.T.astype(jnp.bfloat16)
+            keys.append(rotate(a[:, g * 2 * HEAD:g * 2 * HEAD + HEAD] + small[0:1, col:col + HEAD], c, s))
+            vals.append(a[:, g * 2 * HEAD + HEAD:(g + 1) * 2 * HEAD] + small[0:1, col + HEAD:col + 2 * HEAD])
+            ka[g, pl.ds(at, rows4), :] = keys[g].astype(jnp.bfloat16)
+            vt[g, :, pl.ds(at, rows4)] = vals[g].T.astype(jnp.bfloat16)
+        kv_out[0, rows] = jnp.swapaxes(jnp.stack(keys), 0, 1).astype(jnp.bfloat16)
+        kv_out[1, rows] = jnp.swapaxes(jnp.stack(vals), 0, 1).astype(jnp.bfloat16)
+
+    def kv_step(r, _):
+        x_copy(r + 1).wait()
+
+        @pl.when(r > 0)
+        def _():
+            send_new(r - 1)
+
+        keys_values(r, True)
         return 0
 
-    lax.fori_loop(0, 4, kv_step, 0)
+    x_copy(0).wait()
+    for b in range(nsub):
+        norm(b)
+    lax.fori_loop(0, 3, kv_step, 0)
+    send_new(2)
+    keys_values(3, False)
+    wq_copy(1).start()
     send_new(3)
-    wq_copy(1).start()
 
     def out_copies():
-        res = []
-        for g in range(p.kv):
-            cols = pl.ds(g * HEAD, HEAD)
-            res.append(pltpu.make_async_copy(ka.at[g, pl.ds(new0, p.tok)], kn.at[:, cols], out_sem.at[g]))
-            res.append(pltpu.make_async_copy(vb.at[g], vn.at[:, cols], out_sem.at[p.kv + g]))
-        return res
+        return [pltpu.make_async_copy(kv_out.at[0], kn, out_sem.at[0]), pltpu.make_async_copy(kv_out.at[1], vn, out_sem.at[1])]
 
     for c in out_copies():
         c.start()
@@ -218,8 +228,10 @@
 
     lax.fori_loop(0, p.nd, reset, 0)
 
-    def q_tile(t, first, count):
+    def q_tile(t):
         j = lax.rem(t, p.nq)
+        first = t // p.nq * 2
+        count = 2
         rows = pl.ds(pl.multiple_of(first * p.mr, p.mr), count * p.mr)
         wq_copy(t).wait()
         a = jnp.dot(h[rows, :], w[lax.rem(t, 2)], preferred_element_type=jnp.float32)
@@ -422,7 +434,7 @@
         return pltpu.make_async_copy(x.at[pl.ds(pl.multiple_of(m * p.mr + x_half, p.half), p.half)], xb, b_sem.at[5])
 
     def first_q(t, _):
-        q_tile(t, 0, 1)
+        q_tile(t)
 
         @pl.when(t == max(0, p.nq - 3))
         def _():
@@ -480,13 +492,15 @@
         @pl.when(busy & (s == p.s_fin))
         def _():
             def finish(i, _):
-                inv = 1.0 / jnp.sum(l_s[i], axis=0, keepdims=True)
-                v = o_t[i] * inv
-                for k in range(2):
-                    o[:, pl.ds(pl.multiple_of((i * 2 + k) * HEAD, HEAD), HEAD)] = v[:, k * p.mr:(k + 1) * p.mr].T.astype(jnp.bfloat16)
-                return reset(i, 0)
-
-            lax.fori_loop(0, p.nd, finish, 0)
+                for e in range(p.fin):
+                    c = i * p.fin + e
+                    v = o_t[c] * (1.0 / jnp.sum(l_s[c], axis=0, keepdims=True))
+                    for k in range(2):
+                        o[:, pl.ds(pl.multiple_of((c * 2 + k) * HEAD, HEAD), HEAD)] = v[:, k * p.mr:(k + 1) * p.mr].T.astype(jnp.bfloat16)
+                    reset(c, 0)
+                return 0
+
+            lax.fori_loop(0, p.nd // p.fin, finish, 0)
 
         @pl.when(busy & (s >= p.s_out) & (s < p.s_q))
         def _():
@@ -514,19 +528,9 @@
             own[lax.rem(m, p.owns), n // p.per, 0:p.half, cols] = a[0:p.half] + r * take_a
             own[lax.rem(m, p.owns), n // p.per, p.half:p.mr, cols] = a[p.half:p.mr] + r * take_b
 
-        @pl.when((m == 0) & (s >= p.s_q))
-        def _():
-            for k in range(2):
-                q_tile(p.nq + 2 * (s - p.s_q) + k, 1, 1)
-
-        @pl.when((m == 1) & (s >= p.s_q))
-        def _():
-            for k in range(2):
-                q_tile(2 * p.nq + 2 * (s - p.s_q) + k, 2, 2)
-
-        @pl.when((m >= 2) & (m < p.nm - 2) & (s >= p.s_q))
-        def _():
-            q_tile(3 * p.nq + (m - 2) * p.hq + s - p.s_q, m - lax.rem(m, 2) + 2, 2)
+        @pl.when((m < p.nm - 2) & (s >= p.s_q))
+        def _():
+            q_tile((m // 2 + 1) * p.nq + lax.rem(m, 2) * p.hq + s - p.s_q)
 
         service(seg)
         return 0
@@ -581,25 +585,27 @@
 
 def build(p):
     def local_step(x, k_cache, v_cache, rope_table, norm_gain, w_qkv, b_qkv, w_out):
-        small = jnp.concatenate([b_qkv, norm_gain]).astype(jnp.float32).reshape(1, -1)
-        cached = jnp.stack([k_cache, v_cache]).transpose(0, 2, 1, 3)
         anyspace = pl.BlockSpec(memory_space=pl.ANY)
-        vmem = pl.BlockSpec(memory_space=pltpu.VMEM)
         bf, f32 = jnp.bfloat16, jnp.float32
         dma = pltpu.SemaphoreType.DMA
-        kvw = p.kv * HEAD
-        y, kn, vn, _ = pl.pallas_call(
+        kv_shape = jax.ShapeDtypeStruct((p.tok, p.kv, HEAD), bf)
+        y, k_new, v_new, _ = pl.pallas_call(
             functools.partial(kernel, p),
             name='block',
-            out_shape=(jax.ShapeDtypeStruct((p.tok, p.dim), bf), jax.ShapeDtypeStruct((p.tok, kvw), bf), jax.ShapeDtypeStruct((p.tok, kvw), bf),
+            out_shape=(jax.ShapeDtypeStruct((p.tok, p.dim), bf), kv_shape, kv_shape,
                        jax.ShapeDtypeStruct((2, p.chunks, p.half, p.cc), f32)),
-            in_specs=[anyspace, anyspace, anyspace, vmem, anyspace, anyspace],
+            in_specs=[anyspace] * 8,
             out_specs=(anyspace, anyspace, anyspace, anyspace),
             scratch_shapes=[
                 pltpu.VMEM((p.tok, p.dim), bf),
                 pltpu.VMEM((p.kv, p.keys, HEAD), bf),
                 pltpu.VMEM((p.kv, HEAD, p.keys), bf),
+                pltpu.VMEM((64, p.tok), f32),
                 pltpu.VMEM((p.tok, 64), f32),
+                pltpu.VMEM(((p.group + 2) * p.kv * HEAD,), bf),
+                pltpu.VMEM((p.dim,), bf),
+                pltpu.VMEM((1, (p.group + 2) * p.kv * HEAD + p.dim), f32),
+                pltpu.VMEM((2, p.cache, p.kv, HEAD), bf),
                 pltpu.VMEM((4, p.nd, p.n, HEAD), bf),
                 pltpu.VMEM((p.nd, HEAD, p.n), f32),
                 pltpu.VMEM((p.mr, p.heads * HEAD), bf),
@@ -613,15 +619,14 @@
                 pltpu.VMEM((p.half, p.dim), bf),
                 pltpu.VMEM((2, p.dim, p.wcols), bf),
                 pltpu.VMEM((p.nt, p.heads * HEAD, p.wcols), bf),
-                pltpu.VMEM((p.kv, p.tok, HEAD), bf),
-                dma((4,)), dma((2,)), dma((p.nt,)), dma((6,)), dma((2 * p.kv,)),
+                pltpu.VMEM((2, p.tok, p.kv, HEAD), bf),
+                dma((4,)), dma((2,)), dma((p.nt,)), dma((8,)), dma((2,)),
                 dma((3, 2)), dma((3, 2)), dma((3, 2)), dma((3, 2)),
                 dma((2, p.chunks)), dma((2, p.chunks)), dma((2, 2)), dma((2, p.chunks)), dma((2, p.chunks)), dma((2, p.cpm)),
             ],
             compiler_params=pltpu.CompilerParams(collective_id=0, has_side_effects=True, vmem_limit_bytes=67_000_000),
-        )(x, cached, rope_table, small, w_qkv, w_out)
-        shape = (p.tok, p.kv, HEAD)
-        return y, kn.reshape(shape), vn.reshape(shape)
+        )(x, k_cache, v_cache, rope_table.T, norm_gain, b_qkv, w_qkv, w_out)
+        return y, k_new, v_new
 
     return local_step
 
@@ -630,7 +635,7 @@
     row_spec = P(('dp', 'cp'), None)
     cache_spec = P(('dp', 'cp'), 'tp', None)
     p = Plan(tok=1024, dim=4096, kv=2, group=12, cache=256, nm=8, kt=512)
-    p.table([[8, 14, 16, 19], [15, 17, 20, 22], [19, 22, 27, 33], [31, 35, 38, 40]],
-            [[36, 39, 41, 47], [39, 45, 51, 53], [54, 57, 59, 61]])
+    p.table([[8, 12, 16, 19], [16, 18, 21, 23], [20, 22, 26, 33], [32, 35, 38, 40]],
+            [[35, 39, 42, 46], [38, 44, 52, 53], [54, 57, 58, 60]])
     return jax.shard_map(build(p), mesh=mesh, in_specs=(row_spec, cache_spec, cache_spec, row_spec, P(None), P(None, 'tp'), P('tp'), P('tp', None)),
                          out_specs=(row_spec, cache_spec, cache_spec), check_vma=False)

time: 374 us -> 365 us (0.976)
  local copies, waits for them, and re-layouts: 16.2 us -> 9.57 us
    reshape x2 -> x0, local copies, waits for them, and re-layouts: 3.92 us -> none  [local_step(): return (y, kn.reshape(shape), vn.reshape(shape))]
    unnamed x2 -> x7, local copies, waits for them, and re-layouts: 9.83 us -> 9.57 us
where the time goes in v4:
time: 365 us; the launch traced here: 363 us
  Pallas kernels  353 us (97%)
  local copies, waits for them, and re-layouts  9.57 us (3%)
    pallas_call x1, Pallas kernels, local_step(): pl.pallas_call(functools.partial(kernel, p), name='block', out_shape=(jax...  353 us
    unnamed x7, local copies, waits for them, and re-layouts  9.57 us

profile of v4, /device:TPU:5, one launch (start us, length us, event | category | flops | bytes accessed | tf_op | source)
XLA Modules:
  0.0 363.4 jit_solution(9164949304486842660)
XLA Ops:
  0.6 353.1 %block.1 = (bf16[1024,4096]{1,0:T(8,128)(2,1)}, bf16[1024,2,128]{2,1,0:T(2,128)(2,1)}, bf16[1024,2,128]{2,1,0:T(2,128)(2,1)}, f32[2,32,64,1024]{3,2,1,0:T(8,128)}) custom-call(bf16[1024,4096]{1,0:T(8,128)(2,1)} %x.1, bf16[256,2,128]{2,1,0:T(2,128)(2,1)} %k_in.1, bf16[256,2,128]{2,1,0:T(2,128)(2,1)} %v_in.1, f32[64,1024]{1,0:T(8,128)} %bitcast.1, ...), custom_call_target="tpu_custom_call" | custom-call | tf_op jit(solution)/shard_map/block/pallas_call | solution.py:592
  353.8 0.0 copy-start.1
  353.8 0.0 copy-start
  353.8 8.0 %copy.14 = bf16[1024,4096]{1,0:T(8,128)(2,1)} copy(bf16[1024,4096]{1,0:T(8,128)(2,1)} %get-tuple-element.12) | data formatting | bytes 16777216
  361.8 0.0 copy-done.1
  361.8 0.8 copy.15
  362.6 0.0 copy-done
  362.6 0.8 copy.16
Async XLA Ops:
  353.8 8.0 %copy-start.1 = (bf16[1024,2,128]{2,1,0:T(2,128)(2,1)S(1)}, bf16[1024,2,128]{2,1,0:T(2,128)(2,1)}, u32[]{:S(2)}) copy-start(bf16[1024,2,128]{2,1,0:T(2,128)(2,1)} %get-tuple-element.13) | copy-start | bytes 1572868
  353.8 8.8 %copy-start = (bf16[1024,2,128]{2,1,0:T(2,128)(2,1)S(1)}, bf16[1024,2,128]{2,1,0:T(2,128)(2,1)}, u32[]{:S(2)}) copy-start(bf16[1024,2,128]{2,1,0:T(2,128)(2,1)} %get-tuple-element.14) | copy-start | bytes 1572868

commit v5 on v4

--- a/solution.py
+++ b/solution.py
@@ -31,9 +31,10 @@
         self.qpg = group // QUAD
         self.hq = self.nq // 2
         self.nt = dim // self.wcols
-        self.cpm = 4
-        self.per = self.nt // self.cpm
-        self.cc = dim // self.cpm
+        self.cpm = self.nt
+        self.cc = self.wcols
+        self.ring = self.cpm
+        self.ys = 4
         self.half = self.mr // 2
         self.owns = 2
         self.fin = math.gcd(self.nd, 3)
@@ -45,17 +46,26 @@
         self.s_q = self.s_out + self.nt
         self.nseg = self.s_q + self.hq
         self.chunks = nm * self.cpm
-        self.table([[self.s_out + self.per * (j + 1) - 1 + 3 * r for j in range(self.cpm)] for r in range(4)],
-                   [[self.s_out + self.per * (j + 1) - 1 + 12 + 3 * r for j in range(self.cpm)] for r in range(3)])
+        self.table([[self.s_out + j + 2 * r for j in range(self.cpm)] for r in range(4)],
+                   [[self.s_out + j + 8 + 2 * r for j in range(self.cpm)] for r in range(3)])
 
     def table(self, sums, rows):
-        self.sums, self.rows = sums, rows
         self.total = self.nseg * (self.nm - 1) + max(max(r) for r in sums + rows) + 1
-
-def kernel(p, x, k_in, v_in, rope_in, gain_in, bias_in, wqkv, wout, y, kn, vn, land,
-           h, ka, vt, rope_t, rope, b1, g1, small, cached, q, o_t, o, s_t, mx_t, m_s, l_s, own, stage, yst, xb, w, wo, kv_out,
+        self.sums, self.rows = [self.words(r) for r in sums], [self.words(r) for r in rows]
+
+    def words(self, due):
+        res = [0] * (self.nseg // 5 + 1)
+        for j, at in enumerate(due):
+            rest = at % self.nseg
+            assert res[rest // 5] >> 6 * (rest % 5) & 63 == 0
+            res[rest // 5] += (1 + j + self.cpm * (at // self.nseg)) << 6 * (rest % 5)
+        return res
+
+
+def kernel(p, x, k_in, v_in, rope_in, gain_in, bias_in, wqkv, wout, y, kn, vn,
+           h, ka, vt, rope_t, rope, b1, g1, small, cached, q, o_t, o, s_t, mx_t, m_s, l_s, own, land, yst, xb, w, wo, kv_out,
            x_sem, w_sem, wo_sem, b_sem, out_sem, cs_send, cs_recv, kv_send, kv_recv,
-           rs_send, rs_recv, st_sem, ag_send, ag_recv, yl_sem):
+           rs_send, rs_recv, free_sem, ag_send, ag_recv, yl_sem):
     tp = lax.axis_index('tp')
     cp = lax.axis_index('cp')
     partner = cp + 1 - 2 * lax.rem(cp, 2)
@@ -330,18 +340,15 @@
         mine = own.at[lax.rem(m, p.owns), j, pl.ds(d * p.half, p.half)]
         rows = pl.ds(pl.multiple_of(m * p.mr + d * p.half, p.half), p.half)
         cols = pl.ds(pl.multiple_of(j * p.cc, p.cc), p.cc)
-        return mine, land.at[d, i], y.at[rows, cols]
+        return mine, land.at[d, lax.rem(i, p.ring)], y.at[rows, cols]
 
     def peers(d):
         return (jnp.maximum(tp - 1, 0), jnp.minimum(tp + 1, 3)) if d == 0 else (jnp.minimum(tp + 1, 3), jnp.maximum(tp - 1, 0))
 
     def rs_copy(d, i):
         mine, there, _ = chain(d, i)
-        return pltpu.make_async_remote_copy(mine, there, rs_send.at[d, i], rs_recv.at[d, i], device_id={'tp': peers(d)[0]}, device_id_type=MESH)
-
-    def st_copy(d, i):
-        k = lax.rem(i, 2)
-        return pltpu.make_async_copy(land.at[d, i], stage.at[d, k], st_sem.at[d, k])
+        return pltpu.make_async_remote_copy(mine, there, rs_send.at[d, lax.rem(i, p.owns * p.cpm)], rs_recv.at[d, lax.rem(i, p.ring)],
+                                            device_id={'tp': peers(d)[0]}, device_id_type=MESH)
 
     def ag_copy(d, i, src=None):
         out = chain(d, i)[2]
@@ -349,63 +356,73 @@
                                             device_id={'tp': peers(d)[1]}, device_id_type=MESH)
 
     def yl_copy(d, i):
-        k = lax.rem(i, p.cpm)
+        k = lax.rem(i, p.ys)
         return pltpu.make_async_copy(yst.at[d, k], chain(d, i)[2], yl_sem.at[d, k])
 
-    def pick(role, table, j):
-        v = table[0][j]
-        for r in range(1, len(table)):
-            v = jnp.where(role == r, table[r][j], v)
-        return v
-
-    def when_due(seg, role, table, ahead, act):
-        hit = seg < 0
-        i = 0
-        for j in range(p.cpm):
-            t = seg + ahead - pick(role, table, j)
-            m = jnp.maximum(t, 0) // p.nseg
-            due = (t >= 0) & (m < p.nm) & (lax.rem(jnp.maximum(t, 0), p.nseg) == 0)
-            hit = hit | due
-            i = i + jnp.where(due, m * p.cpm + j, 0)
-
-        @pl.when(hit)
-        def _():
-            act(i)
+    def pick(role, table):
+        res = []
+        for k in range(len(table[0])):
+            v = table[0][k]
+            for r in range(1, len(table)):
+                v = jnp.where(role == r, table[r][k], v)
+            res.append(v)
+        return res
+
+    due = [(d, role, pick(role, p.sums), pick(2 - role, p.rows)) for d, role in ((0, role_a), (1, role_b))]
+
+    def when_due(seg, words, act):
+        rest = lax.rem(seg, p.nseg)
+        w = words[0]
+        for k in range(1, len(words)):
+            w = jnp.where(rest >= 5 * k, words[k], w)
+        code = jnp.bitwise_and(jnp.right_shift(w, 6 * lax.rem(rest, 5)), 63) - 1
+        m = seg // p.nseg - jnp.maximum(code, 0) // p.cpm
+
+        @pl.when((code >= 0) & (m >= 0) & (m < p.nm))
+        def _():
+            act(m * p.cpm + lax.rem(code, p.cpm))
 
     def service(seg):
-        for d, role in ((0, role_a), (1, role_b)):
+        for d, role, sum_words, _ in due:
             def sums(i, d=d, role=role):
-                mine = chain(d, i)[0]
-                arrived = stage.at[d, lax.rem(i, 2)]
+                mine, arrived, _ = chain(d, i)
 
                 @pl.when(role > 0)
                 def _():
-                    st_copy(d, i).wait()
+                    rs_copy(d, i).wait_recv()
 
                 @pl.when((role > 0) & (role < 3))
                 def _():
                     mine[...] = mine[...] + arrived[...]
 
+                @pl.when((role < 3) & (i >= p.ring))
+                def _():
+                    pl.semaphore_wait(free_sem.at[d], 1)
+
                 @pl.when(role < 3)
                 def _():
                     rs_copy(d, i).start()
 
                 @pl.when(role == 3)
                 def _():
-                    k = lax.rem(i, p.cpm)
-
-                    @pl.when(i >= p.cpm)
+                    k = lax.rem(i, p.ys)
+
+                    @pl.when(i >= p.ys)
                     def _():
-                        yl_copy(d, i - p.cpm).wait()
-                        ag_copy(d, i - p.cpm, yst.at[d, k]).wait_send()
+                        yl_copy(d, i - p.ys).wait()
+                        ag_copy(d, i - p.ys, yst.at[d, k]).wait_send()
 
                     yst[d, k] = (mine[...] + arrived[...]).astype(jnp.bfloat16)
                     yl_copy(d, i).start()
                     ag_copy(d, i, yst.at[d, k]).start()
 
-            when_due(seg, role, p.sums, 0, sums)
-
-        for d, role in ((0, role_a), (1, role_b)):
+                @pl.when((role > 0) & (i < p.chunks - p.ring))
+                def _():
+                    pl.semaphore_signal(free_sem.at[d], inc=1, device_id={'tp': peers(d)[1]}, device_id_type=MESH)
+
+            when_due(seg, sum_words, sums)
+
+        for d, role, _, row_words in due:
             def rows(i, d=d, role=role):
                 @pl.when(role < 3)
                 def _():
@@ -415,16 +432,7 @@
                 def _():
                     ag_copy(d, i).start()
 
-            when_due(seg, 2 - role, p.rows, 0, rows)
-
-        for d, role in ((0, role_a), (1, role_b)):
-            def fetch(i, d=d, role=role):
-                @pl.when(role > 0)
-                def _():
-                    rs_copy(d, i).wait_recv()
-                    st_copy(d, i).start()
-
-            when_due(seg, role, p.sums, 1, fetch)
+            when_due(seg, row_words, rows)
 
     take_a = jnp.where(tp == 0, 1, 0).astype(jnp.float32)
     take_b = jnp.where(tp == 3, 1, 0).astype(jnp.float32)
@@ -524,9 +532,8 @@
 
             a = jnp.dot(o[...], wo[n], preferred_element_type=jnp.float32)
             r = xb[:, pl.ds(pl.multiple_of(n * p.wcols, HEAD), p.wcols)].astype(jnp.float32)
-            cols = pl.ds(pl.multiple_of(lax.rem(n, p.per) * p.wcols, HEAD), p.wcols)
-            own[lax.rem(m, p.owns), n // p.per, 0:p.half, cols] = a[0:p.half] + r * take_a
-            own[lax.rem(m, p.owns), n // p.per, p.half:p.mr, cols] = a[p.half:p.mr] + r * take_b
+            own[lax.rem(m, p.owns), n, 0:p.half, :] = a[0:p.half] + r * take_a
+            own[lax.rem(m, p.owns), n, p.half:p.mr, :] = a[p.half:p.mr] + r * take_b
 
         @pl.when((m < p.nm - 2) & (s >= p.s_q))
         def _():
@@ -554,8 +561,8 @@
 
         @pl.when(role == 3)
         def _():
-            for k in range(p.cpm):
-                i = p.chunks - p.cpm + k
+            for k in range(p.ys):
+                i = p.chunks - p.ys + k
                 yl_copy(d, i).wait()
                 ag_copy(d, i, yst.at[d, k]).wait_send()
 
@@ -589,13 +596,12 @@
         bf, f32 = jnp.bfloat16, jnp.float32
         dma = pltpu.SemaphoreType.DMA
         kv_shape = jax.ShapeDtypeStruct((p.tok, p.kv, HEAD), bf)
-        y, k_new, v_new, _ = pl.pallas_call(
+        y, k_new, v_new = pl.pallas_call(
             functools.partial(kernel, p),
             name='block',
-            out_shape=(jax.ShapeDtypeStruct((p.tok, p.dim), bf), kv_shape, kv_shape,
-                       jax.ShapeDtypeStruct((2, p.chunks, p.half, p.cc), f32)),
+            out_shape=(jax.ShapeDtypeStruct((p.tok, p.dim), bf), kv_shape, kv_shape),
             in_specs=[anyspace] * 8,
-            out_specs=(anyspace, anyspace, anyspace, anyspace),
+            out_specs=(anyspace, anyspace, anyspace),
             scratch_shapes=[
                 pltpu.VMEM((p.tok, p.dim), bf),
                 pltpu.VMEM((p.kv, p.keys, HEAD), bf),
@@ -614,15 +620,15 @@
                 pltpu.VMEM((p.nd, 8, p.n), f32),
                 pltpu.VMEM((p.nd, 8, p.n), f32),
                 pltpu.VMEM((p.owns, p.cpm, p.mr, p.cc), f32),
-                pltpu.VMEM((2, 2, p.half, p.cc), f32),
-                pltpu.VMEM((2, p.cpm, p.half, p.cc), bf),
+                pltpu.VMEM((2, p.ring, p.half, p.cc), f32),
+                pltpu.VMEM((2, p.ys, p.half, p.cc), bf),
                 pltpu.VMEM((p.half, p.dim), bf),
                 pltpu.VMEM((2, p.dim, p.wcols), bf),
                 pltpu.VMEM((p.nt, p.heads * HEAD, p.wcols), bf),
                 pltpu.VMEM((2, p.tok, p.kv, HEAD), bf),
                 dma((4,)), dma((2,)), dma((p.nt,)), dma((8,)), dma((2,)),
                 dma((3, 2)), dma((3, 2)), dma((3, 2)), dma((3, 2)),
-                dma((2, p.chunks)), dma((2, p.chunks)), dma((2, 2)), dma((2, p.chunks)), dma((2, p.chunks)), dma((2, p.cpm)),
+                dma((2, p.owns * p.cpm)), dma((2, p.ring)), pltpu.SemaphoreType.REGULAR((2,)), dma((2, p.chunks)), dma((2, p.chunks)), dma((2, p.ys)),
             ],
             compiler_params=pltpu.CompilerParams(collective_id=0, has_side_effects=True, vmem_limit_bytes=67_000_000),
         )(x, k_cache, v_cache, rope_table.T, norm_gain, b_qkv, w_qkv, w_out)
@@ -635,7 +641,7 @@
     row_spec = P(('dp', 'cp'), None)
     cache_spec = P(('dp', 'cp'), 'tp', None)
     p = Plan(tok=1024, dim=4096, kv=2, group=12, cache=256, nm=8, kt=512)
-    p.table([[8, 12, 16, 19], [16, 18, 21, 23], [20, 22, 26, 33], [32, 35, 38, 40]],
-            [[35, 39, 42, 46], [38, 44, 52, 53], [54, 57, 58, 60]])
+    p.table([[7, 10, 15, 16, 17, 19, 20, 21], [15, 17, 19, 20, 21, 22, 23, 28], [18, 20, 21, 22, 23, 27, 32, 33], [20, 22, 24, 29, 32, 34, 35, 37]],
+            [[28, 32, 33, 36, 37, 38, 39, 40], [35, 36, 37, 38, 39, 40, 42, 46], [37, 38, 39, 40, 41, 47, 50, 52]])
     return jax.shard_map(build(p), mesh=mesh, in_specs=(row_spec, cache_spec, cache_spec, row_spec, P(None), P(None, 'tp'), P('tp'), P('tp', None)),
                          out_specs=(row_spec, cache_spec, cache_spec), check_vma=False)

time: 365 us -> 347 us (0.951)
  Pallas kernels: 353 us -> 336 us
    pallas_call x1, Pallas kernels: 353 us -> 336 us  [local_step(): pl.pallas_call(functools.partial(kernel, p), name='block', out_shape=(jax...]
where the time goes in v5:
time: 347 us; the launch traced here: 346 us
  Pallas kernels  336 us (97%)
  local copies, waits for them, and re-layouts  9.57 us (3%)
    pallas_call x1, Pallas kernels, local_step(): pl.pallas_call(functools.partial(kernel, p), name='block', out_shape=(jax...  336 us
    unnamed x7, local copies, waits for them, and re-layouts  9.57 us

profile of v5, /device:TPU:5, one launch (start us, length us, event | category | flops | bytes accessed | tf_op | source)
XLA Modules:
  0.0 346.2 jit_solution(17171945939566948775)
XLA Ops:
  0.6 336.0 %block.1 = (bf16[1024,4096]{1,0:T(8,128)(2,1)}, bf16[1024,2,128]{2,1,0:T(2,128)(2,1)}, bf16[1024,2,128]{2,1,0:T(2,128)(2,1)}) custom-call(bf16[1024,4096]{1,0:T(8,128)(2,1)} %x.1, bf16[256,2,128]{2,1,0:T(2,128)(2,1)} %k_in.1, bf16[256,2,128]{2,1,0:T(2,128)(2,1)} %v_in.1, f32[64,1024]{1,0:T(8,128)} %bitcast.1, bf16[4096]{0:T(1024)(128)(2,1)} %gain_in.1, ...), custom_call_target="tpu_custom_call" | custom-call | tf_op jit(solution)/shard_map/block/pallas_call | solution.py:599
  336.6 0.0 copy-start.1
  336.6 0.0 copy-start
  336.6 8.0 %copy.14 = bf16[1024,4096]{1,0:T(8,128)(2,1)} copy(bf16[1024,4096]{1,0:T(8,128)(2,1)} %get-tuple-element.6) | data formatting | bytes 16777216
  344.6 0.0 copy-done.1
  344.6 0.8 copy.15
  345.4 0.0 copy-done
  345.4 0.8 copy.16
Async XLA Ops:
  336.6 8.0 %copy-start.1 = (bf16[1024,2,128]{2,1,0:T(2,128)(2,1)S(1)}, bf16[1024,2,128]{2,1,0:T(2,128)(2,1)}, u32[]{:S(2)}) copy-start(bf16[1024,2,128]{2,1,0:T(2,128)(2,1)} %get-tuple-element.7) | copy-start | bytes 1572868
  336.6 8.8 %copy-start = (bf16[1024,2,128]{2,1,0:T(2,128)(2,1)S(1)}, bf16[1024,2,128]{2,1,0:T(2,128)(2,1)}, u32[]{:S(2)}) copy-start(bf16[1024,2,128]{2,1,0:T(2,128)(2,1)} %get-tuple-element.8) | copy-start | bytes 1572868

commit v6 on v5

--- a/solution.py
+++ b/solution.py
@@ -138,7 +138,7 @@
     def send_new(r):
         at = pl.multiple_of(new0 + r * rows4, rows4)
 
-        @pl.when(cp < 2)
+        @pl.when(cp == 0)
         def _():
             for c in new_copies(at, rows4, across, 1):
                 c.start()
@@ -170,7 +170,7 @@
     for r in range(1, 4):
         x_copy(r).start()
     wq_copy(0).start()
-    nsub = max(1, rows4 // 128)
+    nsub = max(8, rows4 // 32)
     sub = rows4 // nsub
     wide = 512
 
@@ -190,10 +190,15 @@
     def keys_values(r, ahead):
         rows = pl.ds(pl.multiple_of(r * rows4, rows4), rows4)
         at = pl.multiple_of(new0 + r * rows4, rows4)
-        a = jnp.dot(h[rows, :], w[1], preferred_element_type=jnp.float32)
-        if ahead:
-            for b in range(nsub):
-                norm((r + 1) * nsub + b)
+        a = None
+        per = nsub // 8
+        deep = p.dim // 8
+        for e in range(8):
+            part = jnp.dot(h[rows, e * deep:(e + 1) * deep], w[1, e * deep:(e + 1) * deep, :], preferred_element_type=jnp.float32)
+            a = part if a is None else a + part
+            if ahead:
+                for b in range(per):
+                    norm((r + 1) * nsub + e * per + b)
         c, s = angles(rows, rows4)
         keys, vals = [], []
         for g in range(p.kv):
@@ -223,6 +228,11 @@
     keys_values(3, False)
     wq_copy(1).start()
     send_new(3)
+
+    @pl.when(cp == 1)
+    def _():
+        for c in new_copies(new0, p.tok, across, 1):
+            c.start()
 
     def out_copies():
         return [pltpu.make_async_copy(kv_out.at[0], kn, out_sem.at[0]), pltpu.make_async_copy(kv_out.at[1], vn, out_sem.at[1])]
@@ -312,7 +322,7 @@
             weigh(i, own_at(j), i % slots)
 
     def block_at(b):
-        return jnp.where(b == 0, 0, p.tok * (1 + jnp.where(lax.rem(cp, 2) == 1, cp - b, b - 1)))
+        return jnp.where(b == 0, 0, p.tok * (1 + jnp.where((cp == 3) & (b == 1), 2, jnp.where(cp == 3, b - 2, b - 1))))
 
     def block_segment(u, b, count):
         qs = lax.rem(u, 4)
@@ -480,17 +490,23 @@
             for c in new_copies(pl.multiple_of(p.tok * cp, p.tok), p.tok, partner, 0):
                 c.wait_recv()
 
+        direct = pl.multiple_of(p.tok * jnp.maximum(cp - 1, 0), p.tok)
+
+        @pl.when((cp == 3) & (seg == p.s_blk + 2))
+        def _():
+            for c in new_copies(direct, p.tok, partner, 2):
+                c.wait_recv()
+
         @pl.when((cp >= 2) & (seg == p.s_blk + cp - 1))
         def _():
-            direct = pl.multiple_of(p.tok * (cp - 1), p.tok)
             for c in new_copies(direct, p.tok, partner, 1):
                 c.wait_recv()
             for c in new_copies(direct, p.tok, partner, 2):
                 c.start()
 
-        @pl.when((cp >= 2) & (seg == p.s_blk + cp))
-        def _():
-            for c in new_copies(pl.multiple_of(p.tok * (cp - 1), p.tok), p.tok, partner, 2):
+        @pl.when((cp == 2) & (seg == p.s_blk + 2))
+        def _():
+            for c in new_copies(direct, p.tok, partner, 2):
                 c.wait_recv()
 
         @pl.when(busy & (s >= p.s_blk) & (s < p.s_blk + blocks))
@@ -588,6 +604,26 @@
     def _():
         for c in new_copies(pl.multiple_of(p.tok * (cp - 1), p.tok), p.tok, partner, 2):
             c.wait_send()
+
+
+def settle(pieces, *refs):
+    n = len(pieces)
+    src, dst, hold, sems = refs[:n], refs[n:2 * n], refs[2 * n:3 * n], refs[3 * n]
+    into, out = [], []
+    for a, count in enumerate(pieces):
+        rows = src[a].shape[0] // count
+        for k in range(count):
+            at = pl.ds(k * rows, rows)
+            i = len(into)
+            into.append(pltpu.make_async_copy(src[a].at[at], hold[a].at[at], sems.at[0, i]))
+            out.append(pltpu.make_async_copy(hold[a].at[at], dst[a].at[at], sems.at[1, i]))
+    for c in into:
+        c.start()
+    for c, d in zip(into, out):
+        c.wait()
+        d.start()
+    for d in out:
+        d.wait()
 
 
 def build(p):
@@ -632,7 +668,17 @@
             ],
             compiler_params=pltpu.CompilerParams(collective_id=0, has_side_effects=True, vmem_limit_bytes=67_000_000),
         )(x, k_cache, v_cache, rope_table.T, norm_gain, b_qkv, w_qkv, w_out)
-        return y, k_new, v_new
+        res = (y, k_new, v_new)
+        pieces = (16, 1, 1)
+        return pl.pallas_call(
+            functools.partial(settle, pieces),
+            name='settle',
+            out_shape=tuple(jax.ShapeDtypeStruct(r.shape, r.dtype) for r in res),
+            in_specs=[anyspace] * 3,
+            out_specs=(anyspace,) * 3,
+            scratch_shapes=[pltpu.VMEM(r.shape, r.dtype) for r in res] + [dma((2, sum(pieces)))],
+            compiler_params=pltpu.CompilerParams(vmem_limit_bytes=67_000_000),
+        )(*res)
 
     return local_step
 

time: 347 us -> 344 us (level)
  local copies, waits for them, and re-layouts: 9.57 us -> 0 us
  Pallas kernels: 336 us -> 343 us
    unnamed x7 -> x0, local copies, waits for them, and re-layouts: 9.57 us -> none
    pallas_call x0 -> x1, Pallas kernels: none -> 7.52 us  [local_step(): pl.pallas_call(functools.partial(settle, pieces), name='settle', out_shap...]
where the time goes in v6:
time: 344 us
  Pallas kernels  343 us (100%)
    pallas_call x1, Pallas kernels, local_step(): pl.pallas_call(functools.partial(kernel, p), name='block', out_shape=(jax...  336 us
    pallas_call x1, Pallas kernels, local_step(): pl.pallas_call(functools.partial(settle, pieces), name='settle', out_shap...  7.52 us

profile of v6, /device:TPU:5, one launch (start us, length us, event | category | flops | bytes accessed | tf_op | source)
XLA Modules:
  0.0 343.8 jit_solution(5840957729538786729)
XLA Ops:
  0.6 335.7 %block.1 = (bf16[1024,4096]{1,0:T(8,128)(2,1)}, bf16[1024,2,128]{2,1,0:T(2,128)(2,1)}, bf16[1024,2,128]{2,1,0:T(2,128)(2,1)}) custom-call(bf16[1024,4096]{1,0:T(8,128)(2,1)} %x.1, bf16[256,2,128]{2,1,0:T(2,128)(2,1)} %k_in.1, bf16[256,2,128]{2,1,0:T(2,128)(2,1)} %v_in.1, f32[64,1024]{1,0:T(8,128)} %bitcast.1, bf16[4096]{0:T(1024)(128)(2,1)} %gain_in.1, ...), custom_call_target="tpu_custom_call" | custom-call | tf_op jit(solution)/shard_map/block/pallas_call | solution.py:635
  336.3 7.5 %settle.1 = (bf16[1024,4096]{1,0:T(8,128)(2,1)}, bf16[1024,2,128]{2,1,0:T(2,128)(2,1)}, bf16[1024,2,128]{2,1,0:T(2,128)(2,1)}) custom-call(bf16[1024,4096]{1,0:T(8,128)(2,1)} %get-tuple-element.6.refs_0_, bf16[1024,2,128]{2,1,0:T(2,128)(2,1)} %get-tuple-element.7.refs_1_, bf16[1024,2,128]{2,1,0:T(2,128)(2,1)} %get-tuple-element.8.refs_2_), custom_call_target="tpu_custom_call" | custom-call | tf_op jit(solution)/shard_map/settle/pallas_call | solution.py:673

commit v7 on v6

--- a/solution.py
+++ b/solution.py
@@ -39,6 +39,7 @@
         self.owns = 2
         self.fin = math.gcd(self.nd, 3)
         self.look = 3
+        self.guest = (nm // 2 - 1) * self.cpm + self.cpm - 1
         self.wt = self.nq * (nm // 2)
         self.s_blk = 2
         self.s_fin = self.s_blk + 4
@@ -52,6 +53,11 @@
     def table(self, sums, rows):
         self.total = self.nseg * (self.nm - 1) + max(max(r) for r in sums + rows) + 1
         self.sums, self.rows = [self.words(r) for r in sums], [self.words(r) for r in rows]
+        first = self.guest // self.cpm * self.nseg + self.s_out + self.cpm - 1
+        step = self.nseg // 3
+        self.g_out = first
+        self.g_sums = [first + self.nseg - step + step * r for r in range(4)]
+        self.g_rows = [self.g_sums[3] + step * (r + 1) for r in range(3)]
 
     def words(self, due):
         res = [0] * (self.nseg // 5 + 1)
@@ -63,9 +69,9 @@
 
 
 def kernel(p, x, k_in, v_in, rope_in, gain_in, bias_in, wqkv, wout, y, kn, vn,
-           h, ka, vt, rope_t, rope, b1, g1, small, cached, q, o_t, o, s_t, mx_t, m_s, l_s, own, land, yst, xb, w, wo, kv_out,
+           h, ka, vt, rope_t, rope, b1, g1, small, q, o_t, o, s_t, mx_t, m_s, l_s, own, land, yst, g_in, g_land, g_y, xb, w, wo, kv_out,
            x_sem, w_sem, wo_sem, b_sem, out_sem, cs_send, cs_recv, kv_send, kv_recv,
-           rs_send, rs_recv, free_sem, ag_send, ag_recv, yl_sem):
+           rs_send, rs_recv, free_sem, ag_send, ag_recv, yl_sem, g_send, g_recv):
     tp = lax.axis_index('tp')
     cp = lax.axis_index('cp')
     partner = cp + 1 - 2 * lax.rem(cp, 2)
@@ -97,8 +103,8 @@
     x_copy(0).start()
     for g in range(p.kv):
         wkv_copy(g).start()
-    little = [pltpu.make_async_copy(rope_in, rope_t, b_sem.at[2]), pltpu.make_async_copy(k_in, cached.at[0], b_sem.at[3]),
-              pltpu.make_async_copy(v_in, cached.at[1], b_sem.at[4]), pltpu.make_async_copy(bias_in, b1, b_sem.at[6]),
+    little = [pltpu.make_async_copy(rope_in, rope_t, b_sem.at[2]), pltpu.make_async_copy(k_in, kv_out.at[0, pl.ds(0, p.cache)], b_sem.at[3]),
+              pltpu.make_async_copy(v_in, kv_out.at[1, pl.ds(0, p.cache)], b_sem.at[4]), pltpu.make_async_copy(bias_in, b1, b_sem.at[6]),
               pltpu.make_async_copy(gain_in, g1, b_sem.at[7])]
     for c in little:
         c.start()
@@ -121,19 +127,21 @@
         return (pltpu.make_async_remote_copy(ks, ks, kv_send.at[k, 0], kv_recv.at[k, 0], device_id={'cp': peer}, device_id_type=MESH),
                 pltpu.make_async_remote_copy(vs, vs, kv_send.at[k, 1], kv_recv.at[k, 1], device_id={'cp': peer}, device_id_type=MESH))
 
-    for c in little:
-        c.wait()
+    little[1].wait()
+    little[2].wait()
     here = pl.multiple_of(cp * p.cache, p.cache)
     for g in range(p.kv):
-        ka[g, pl.ds(here, p.cache), :] = cached[0].astype(jnp.float32)[:, g, :].astype(jnp.bfloat16)
-        vt[g, :, pl.ds(here, p.cache)] = cached[1].astype(jnp.float32)[:, g, :].T.astype(jnp.bfloat16)
-    small[0:1, 0:goff] = b1[...].astype(jnp.float32).reshape(1, goff)
-    small[0:1, goff:goff + p.dim] = g1[...].astype(jnp.float32).reshape(1, p.dim)
-    rope[...] = rope_t[...].T
+        ka[g, pl.ds(here, p.cache), :] = kv_out[0, 0:p.cache].astype(jnp.float32)[:, g, :].astype(jnp.bfloat16)
+        vt[g, :, pl.ds(here, p.cache)] = kv_out[1, 0:p.cache].astype(jnp.float32)[:, g, :].T.astype(jnp.bfloat16)
     pl.semaphore_wait(barrier, 6)
     for peer, k in ((across, 1), (partner, 0)):
         for c in cache_copies(cp, peer, k):
             c.start()
+    for c in (little[0], little[3], little[4]):
+        c.wait()
+    small[0:1, 0:goff] = b1[...].astype(jnp.float32).reshape(1, goff)
+    small[0:1, goff:goff + p.dim] = g1[...].astype(jnp.float32).reshape(1, p.dim)
+    rope[...] = rope_t[...].T
 
     def send_new(r):
         at = pl.multiple_of(new0 + r * rows4, rows4)
@@ -369,6 +377,21 @@
         k = lax.rem(i, p.ys)
         return pltpu.make_async_copy(yst.at[d, k], chain(d, i)[2], yl_sem.at[d, k])
 
+    def guest_copy(src, dst, k, d, peer):
+        return pltpu.make_async_remote_copy(src, dst, g_send.at[k, d], g_recv.at[k, d], device_id=peer, device_id_type=MESH)
+
+    def guest_out(d):
+        return guest_copy(chain(d, p.guest)[0], g_in.at[d], 0, d, {'cp': across})
+
+    def guest_sum(d):
+        return guest_copy(g_in.at[d], g_land.at[d], 1, d, {'tp': peers(d)[0]})
+
+    def guest_row(d):
+        return guest_copy(g_y.at[d], g_y.at[d], 2, d, {'tp': peers(d)[1]})
+
+    def guest_home(d):
+        return guest_copy(g_y.at[d], chain(d, p.guest)[2], 3, d, {'cp': across})
+
     def pick(role, table):
         res = []
         for k in range(len(table[0])):
@@ -396,12 +419,13 @@
         for d, role, sum_words, _ in due:
             def sums(i, d=d, role=role):
                 mine, arrived, _ = chain(d, i)
-
-                @pl.when(role > 0)
+                stays = (cp < 2) | (i != p.guest)
+
+                @pl.when((role > 0) & stays)
                 def _():
                     rs_copy(d, i).wait_recv()
 
-                @pl.when((role > 0) & (role < 3))
+                @pl.when((role > 0) & (role < 3) & stays)
                 def _():
                     mine[...] = mine[...] + arrived[...]
 
@@ -409,19 +433,19 @@
                 def _():
                     pl.semaphore_wait(free_sem.at[d], 1)
 
-                @pl.when(role < 3)
+                @pl.when((role < 3) & stays)
                 def _():
                     rs_copy(d, i).start()
 
-                @pl.when(role == 3)
-                def _():
-                    k = lax.rem(i, p.ys)
-
-                    @pl.when(i >= p.ys)
-                    def _():
-                        yl_copy(d, i - p.ys).wait()
-                        ag_copy(d, i - p.ys, yst.at[d, k]).wait_send()
-
+                k = lax.rem(i, p.ys)
+
+                @pl.when((role == 3) & (i >= p.ys) & ((cp < 2) | (i - p.ys != p.guest)))
+                def _():
+                    yl_copy(d, i - p.ys).wait()
+                    ag_copy(d, i - p.ys, yst.at[d, k]).wait_send()
+
+                @pl.when((role == 3) & stays)
+                def _():
                     yst[d, k] = (mine[...] + arrived[...]).astype(jnp.bfloat16)
                     yl_copy(d, i).start()
                     ag_copy(d, i, yst.at[d, k]).start()
@@ -434,15 +458,46 @@
 
         for d, role, _, row_words in due:
             def rows(i, d=d, role=role):
-                @pl.when(role < 3)
+                stays = (cp < 2) | (i != p.guest)
+
+                @pl.when((role < 3) & stays)
                 def _():
                     ag_copy(d, i).wait_recv()
 
-                @pl.when((role < 3) & (role > 0))
+                @pl.when((role < 3) & (role > 0) & stays)
                 def _():
                     ag_copy(d, i).start()
 
             when_due(seg, row_words, rows)
+
+        @pl.when((cp >= 2) & (seg == p.g_out))
+        def _():
+            for d in range(2):
+                guest_out(d).start()
+
+        for d, role, _, _ in due:
+            for r in range(4):
+                @pl.when((cp < 2) & (role == r) & (seg == p.g_sums[r]))
+                def _():
+                    guest_out(d).wait_recv()
+                    if r > 0:
+                        guest_sum(d).wait_recv()
+                    if r < 3:
+                        if r > 0:
+                            g_in[d] = g_in[d] + g_land[d]
+                        guest_sum(d).start()
+                    else:
+                        g_y[d] = (g_in[d] + g_land[d]).astype(jnp.bfloat16)
+                        guest_row(d).start()
+                        guest_home(d).start()
+
+            for r in range(3):
+                @pl.when((cp < 2) & (role == 2 - r) & (seg == p.g_rows[r]))
+                def _():
+                    guest_row(d).wait_recv()
+                    if r < 2:
+                        guest_row(d).start()
+                    guest_home(d).start()
 
     take_a = jnp.where(tp == 0, 1, 0).astype(jnp.float32)
     take_b = jnp.where(tp == 3, 1, 0).astype(jnp.float32)
@@ -537,10 +592,17 @@
             @pl.when((n == 0) & (m >= p.owns))
             def _():
                 for d, role in ((0, role_a), (1, role_b)):
-                    @pl.when(role < 3)
-                    def _():
-                        for j in range(p.cpm):
-                            rs_copy(d, (m - p.owns) * p.cpm + j).wait_send()
+                    for j in range(p.cpm):
+                        i = (m - p.owns) * p.cpm + j
+
+                        @pl.when((role < 3) & ((cp < 2) | (i != p.guest)))
+                        def _():
+                            rs_copy(d, i).wait_send()
+
+                        if j == p.guest % p.cpm:
+                            @pl.when((cp >= 2) & (i == p.guest))
+                            def _():
+                                guest_out(d).wait_send()
 
             @pl.when(m == 0)
             def _():
@@ -571,7 +633,9 @@
         @pl.when((role > 0) & (role < 3))
         def _():
             def last_rows(i, _):
-                ag_copy(d, i).wait_send()
+                @pl.when((cp < 2) | (i != p.guest))
+                def _():
+                    ag_copy(d, i).wait_send()
                 return 0
             lax.fori_loop(0, p.chunks, last_rows, 0)
 
@@ -581,6 +645,23 @@
                 i = p.chunks - p.ys + k
                 yl_copy(d, i).wait()
                 ag_copy(d, i, yst.at[d, k]).wait_send()
+
+    for d, role in ((0, role_a), (1, role_b)):
+        @pl.when(cp >= 2)
+        def _():
+            guest_home(d).wait_recv()
+
+        @pl.when((cp < 2) & (role < 3))
+        def _():
+            guest_sum(d).wait_send()
+
+        @pl.when((cp < 2) & (role > 0))
+        def _():
+            guest_row(d).wait_send()
+
+        @pl.when(cp < 2)
+        def _():
+            guest_home(d).wait_send()
 
     for c in out_copies():
         c.wait()
@@ -647,7 +728,6 @@
                 pltpu.VMEM(((p.group + 2) * p.kv * HEAD,), bf),
                 pltpu.VMEM((p.dim,), bf),
                 pltpu.VMEM((1, (p.group + 2) * p.kv * HEAD + p.dim), f32),
-                pltpu.VMEM((2, p.cache, p.kv, HEAD), bf),
                 pltpu.VMEM((4, p.nd, p.n, HEAD), bf),
                 pltpu.VMEM((p.nd, HEAD, p.n), f32),
                 pltpu.VMEM((p.mr, p.heads * HEAD), bf),
@@ -658,6 +738,9 @@
                 pltpu.VMEM((p.owns, p.cpm, p.mr, p.cc), f32),
                 pltpu.VMEM((2, p.ring, p.half, p.cc), f32),
                 pltpu.VMEM((2, p.ys, p.half, p.cc), bf),
+                pltpu.VMEM((2, p.half, p.cc), f32),
+                pltpu.VMEM((2, p.half, p.cc), f32),
+                pltpu.VMEM((2, p.half, p.cc), bf),
                 pltpu.VMEM((p.half, p.dim), bf),
                 pltpu.VMEM((2, p.dim, p.wcols), bf),
                 pltpu.VMEM((p.nt, p.heads * HEAD, p.wcols), bf),
@@ -665,6 +748,7 @@
                 dma((4,)), dma((2,)), dma((p.nt,)), dma((8,)), dma((2,)),
                 dma((3, 2)), dma((3, 2)), dma((3, 2)), dma((3, 2)),
                 dma((2, p.owns * p.cpm)), dma((2, p.ring)), pltpu.SemaphoreType.REGULAR((2,)), dma((2, p.chunks)), dma((2, p.chunks)), dma((2, p.ys)),
+                dma((4, 2)), dma((4, 2)),
             ],
             compiler_params=pltpu.CompilerParams(collective_id=0, has_side_effects=True, vmem_limit_bytes=67_000_000),
         )(x, k_cache, v_cache, rope_table.T, norm_gain, b_qkv, w_qkv, w_out)
@@ -687,7 +771,7 @@
     row_spec = P(('dp', 'cp'), None)
     cache_spec = P(('dp', 'cp'), 'tp', None)
     p = Plan(tok=1024, dim=4096, kv=2, group=12, cache=256, nm=8, kt=512)
-    p.table([[7, 10, 15, 16, 17, 19, 20, 21], [15, 17, 19, 20, 21, 22, 23, 28], [18, 20, 21, 22, 23, 27, 32, 33], [20, 22, 24, 29, 32, 34, 35, 37]],
-            [[28, 32, 33, 36, 37, 38, 39, 40], [35, 36, 37, 38, 39, 40, 42, 46], [37, 38, 39, 40, 41, 47, 50, 52]])
+    p.table([[7, 9, 14, 15, 17, 19, 20, 21], [14, 16, 18, 19, 20, 21, 22, 23], [17, 18, 20, 21, 22, 23, 25, 30], [20, 22, 23, 24, 27, 30, 34, 36]],
+            [[22, 24, 25, 29, 34, 35, 37, 38], [30, 33, 34, 35, 37, 38, 39, 40], [37, 39, 40, 41, 42, 44, 48, 51]])
     return jax.shard_map(build(p), mesh=mesh, in_specs=(row_spec, cache_spec, cache_spec, row_spec, P(None), P(None, 'tp'), P('tp'), P('tp', None)),
                          out_specs=(row_spec, cache_spec, cache_spec), check_vma=False)

time: 344 us -> 356 us (1.035); the launches traced: 344 us -> 350 us
  Pallas kernels: 343 us -> 350 us
    pallas_call x1, Pallas kernels: 336 us -> 342 us  [local_step(): pl.pallas_call(functools.partial(kernel, p), name='block', out_shape=(jax...]
where the time goes in v7:
time: 356 us; the launch traced here: 350 us
  Pallas kernels  350 us (98%)
    pallas_call x1, Pallas kernels, local_step(): pl.pallas_call(functools.partial(kernel, p), name='block', out_shape=(jax...  342 us
    pallas_call x1, Pallas kernels, local_step(): pl.pallas_call(functools.partial(settle, pieces), name='settle', out_shap...  7.52 us

profile of v7, /device:TPU:5, one launch (start us, length us, event | category | flops | bytes accessed | tf_op | source)
XLA Modules:
  0.0 350.3 jit_solution(4997060310908772182)
XLA Ops:
  0.6 342.0 %block.1 = (bf16[1024,4096]{1,0:T(8,128)(2,1)}, bf16[1024,2,128]{2,1,0:T(2,128)(2,1)}, bf16[1024,2,128]{2,1,0:T(2,128)(2,1)}) custom-call(bf16[1024,4096]{1,0:T(8,128)(2,1)} %x.1, bf16[256,2,128]{2,1,0:T(2,128)(2,1)} %k_in.1, bf16[256,2,128]{2,1,0:T(2,128)(2,1)} %v_in.1, f32[64,1024]{1,0:T(8,128)} %bitcast.1, bf16[4096]{0:T(1024)(128)(2,1)} %gain_in.1, ...), custom_call_target="tpu_custom_call" | custom-call | tf_op jit(solution)/shard_map/block/pallas_call | solution.py:716
  342.6 7.5 %settle.1 = (bf16[1024,4096]{1,0:T(8,128)(2,1)}, bf16[1024,2,128]{2,1,0:T(2,128)(2,1)}, bf16[1024,2,128]{2,1,0:T(2,128)(2,1)}) custom-call(bf16[1024,4096]{1,0:T(8,128)(2,1)} %get-tuple-element.6.refs_0_, bf16[1024,2,128]{2,1,0:T(2,128)(2,1)} %get-tuple-element.7.refs_1_, bf16[1024,2,128]{2,1,0:T(2,128)(2,1)} %get-tuple-element.8.refs_2_), custom_call_target="tpu_custom_call" | custom-call | tf_op jit(solution)/shard_map/settle/pallas_call | solution.py:757

commit v8 on v7

--- a/solution.py
+++ b/solution.py
@@ -771,7 +771,7 @@
     row_spec = P(('dp', 'cp'), None)
     cache_spec = P(('dp', 'cp'), 'tp', None)
     p = Plan(tok=1024, dim=4096, kv=2, group=12, cache=256, nm=8, kt=512)
-    p.table([[7, 9, 14, 15, 17, 19, 20, 21], [14, 16, 18, 19, 20, 21, 22, 23], [17, 18, 20, 21, 22, 23, 25, 30], [20, 22, 23, 24, 27, 30, 34, 36]],
-            [[22, 24, 25, 29, 34, 35, 37, 38], [30, 33, 34, 35, 37, 38, 39, 40], [37, 39, 40, 41, 42, 44, 48, 51]])
+    p.table([[7, 10, 15, 16, 17, 19, 20, 21], [15, 17, 19, 20, 21, 22, 23, 28], [18, 20, 21, 22, 23, 27, 32, 33], [20, 22, 24, 29, 32, 34, 35, 37]],
+            [[28, 32, 33, 36, 37, 38, 39, 40], [35, 36, 37, 38, 39, 40, 42, 46], [37, 38, 39, 40, 41, 47, 50, 52]])
     return jax.shard_map(build(p), mesh=mesh, in_specs=(row_spec, cache_spec, cache_spec, row_spec, P(None), P(None, 'tp'), P('tp'), P('tp', None)),
                          out_specs=(row_spec, cache_spec, cache_spec), check_vma=False)

time: 356 us -> 351 us (0.986); the launches traced: 350 us -> 351 us
  no operation moved by 1% of the time
where the time goes in v8:
time: 351 us
  Pallas kernels  350 us (100%)
    pallas_call x1, Pallas kernels, local_step(): pl.pallas_call(functools.partial(kernel, p), name='block', out_shape=(jax...  342 us
    pallas_call x1, Pallas kernels, local_step(): pl.pallas_call(functools.partial(settle, pieces), name='settle', out_shap...  7.52 us

profile of v8, /device:TPU:5, one launch (start us, length us, event | category | flops | bytes accessed | tf_op | source)
XLA Modules:
  0.0 350.8 jit_solution(6704473621306103061)
XLA Ops:
  0.6 342.5 %block.1 = (bf16[1024,4096]{1,0:T(8,128)(2,1)}, bf16[1024,2,128]{2,1,0:T(2,128)(2,1)}, bf16[1024,2,128]{2,1,0:T(2,128)(2,1)}) custom-call(bf16[1024,4096]{1,0:T(8,128)(2,1)} %x.1, bf16[256,2,128]{2,1,0:T(2,128)(2,1)} %k_in.1, bf16[256,2,128]{2,1,0:T(2,128)(2,1)} %v_in.1, f32[64,1024]{1,0:T(8,128)} %bitcast.1, bf16[4096]{0:T(1024)(128)(2,1)} %gain_in.1, ...), custom_call_target="tpu_custom_call" | custom-call | tf_op jit(solution)/shard_map/block/pallas_call | solution.py:716
  343.1 7.5 %settle.1 = (bf16[1024,4096]{1,0:T(8,128)(2,1)}, bf16[1024,2,128]{2,1,0:T(2,128)(2,1)}, bf16[1024,2,128]{2,1,0:T(2,128)(2,1)}) custom-call(bf16[1024,4096]{1,0:T(8,128)(2,1)} %get-tuple-element.6.refs_0_, bf16[1024,2,128]{2,1,0:T(2,128)(2,1)} %get-tuple-element.7.refs_1_, bf16[1024,2,128]{2,1,0:T(2,128)(2,1)} %get-tuple-element.8.refs_2_), custom_call_target="tpu_custom_call" | custom-call | tf_op jit(solution)/shard_map/settle/pallas_call | solution.py:757
